TPU v7x, 128 devices: a whole 4x4x4 slice. The times are simulated.
128 devices in a mesh: leaf: 32 (over x, y, core), nbr: 4 (over z).
Axes of the slice: x: 4, y: 4, z: 4, core: 2. Of those that a mesh axis runs over, the one named last changes fastest.
Arguments:
- points: bfloat16 [1024, 32, 512], P('leaf'), may hold values from -1.1953125 to 1.1953125
- charges: bfloat16 [1024, 64, 512], P('leaf'), may hold values from -1.5 to 1.5
- projection: bfloat16 [1024, 256, 512], P('leaf', 'nbr'), may hold values from -0.25 to 0.25
- skeleton_index: int32 [1024, 256], P('leaf'), may hold values from 0 to 511, as said below
- near_ids: int32 [1024, 8], P('leaf', 'nbr'), may hold values from 0 to 1023, as said below
- far_ids: int32 [1024, 16], P('leaf', 'nbr'), may hold values from 0 to 1023, as said below
Outputs:
- potentials: float32 [1024, 64, 512], P('leaf', None, 'nbr')
Inputs may be any that keep to these rules, and one draw needn't show every extreme that they name: `skeleton_index`: each row holds 256 different point numbers of its leaf. `near_ids`: take the rows of one block of 32 leaves (leaf numbers k * 32 to k * 32 + 31) and one of the 4 equal groups of columns: at most 3 of its entries name leaves of any one such block, and some block is named exactly 3 times. `far_ids`: take the rows of one block of 32 leaves and one of the 4 equal groups of columns: at most 5 of its entries name leaves of any one such block, and some block is named exactly 5 times.
All inputs are finite; a program needn't handle non-finite values.
Results may differ from a plain program's by a relative error of at most 0.002.
Values may be sent and summed in bfloat16 or wider, within the bound.
A program may use at most 128 MiB of HBM per device.

v0:
```python
import math

import jax
import jax.numpy as jnp
from jax import lax
from jax.sharding import PartitionSpec as P

GAMMA = 1.0


def kernel_terms(targets, sources, weights):
    target_f32 = targets.astype(jnp.float32)
    source_f32 = sources.astype(jnp.float32)
    inner_terms = jnp.einsum("dt,dm->tm", targets, sources, preferred_element_type=jnp.float32)
    distance = (
        jnp.sum(target_f32 * target_f32, axis=0)[:, None]
        + jnp.sum(source_f32 * source_f32, axis=0)[None, :]
        - 2.0 * inner_terms
    )
    kernel = jnp.exp(-GAMMA * distance)
    return jnp.einsum(
        "rm,tm->rt",
        weights.astype(jnp.float32),
        kernel,
        precision=lax.Precision.HIGHEST,
        preferred_element_type=jnp.float32,
    )


def group_terms(targets, sources, weights):
    item_count = targets.shape[0]
    column_count = sources.shape[2]
    block_rows = math.gcd(item_count, max(1, 8192 // column_count))
    steps_count = item_count // block_rows

    def run_block(batch_rows):
        return jax.vmap(kernel_terms)(batch_rows[0], batch_rows[1], batch_rows[2])

    stacked = (
        targets.reshape((steps_count, block_rows) + targets.shape[1:]),
        sources.reshape((steps_count, block_rows) + sources.shape[1:]),
        weights.reshape((steps_count, block_rows) + weights.shape[1:]),
    )
    result = lax.map(run_block, stacked)
    return result.reshape((item_count,) + result.shape[2:])


def slot_plan(id_block, capacity, groups, leaf_dev):
    flat_ids = id_block.reshape(-1)
    owners = flat_ids // leaf_dev
    local_leaf = flat_ids % leaf_dev
    member = (owners[:, None] == jnp.arange(groups, dtype=jnp.int32)[None, :]).astype(jnp.int32)
    before = jnp.cumsum(member, axis=0) - member
    rank_slot = jnp.sum(before * member, axis=1)
    return (local_leaf, owners * capacity + rank_slot)


def slot_table(values, slot_ids, capacity, groups):
    matches = slot_ids[:, None] == jnp.arange(groups * capacity, dtype=jnp.int32)[None, :]
    return jnp.sum(jnp.where(matches, values[:, None], 0), axis=0).reshape(groups, capacity)


def gather_entries(received, slot_ids, leaf_dev):
    flat_rows = received.reshape((-1,) + received.shape[2:])
    picked = flat_rows[slot_ids]
    per_target = slot_ids.shape[0] // leaf_dev
    picked = picked.reshape(leaf_dev, per_target, picked.shape[1], picked.shape[2])
    return picked.transpose(0, 2, 1, 3).reshape(
        leaf_dev, picked.shape[2], per_target * picked.shape[3]
    )


def per_device(points, charges, projection, skeleton_index, near_ids, far_ids):
    leaf_dev = points.shape[0]
    groups = lax.axis_size("leaf")
    near_dev = near_ids.shape[1]
    far_dev = far_ids.shape[1]
    cap_near = max(2, (5 * leaf_dev * near_dev + 4 * groups - 1) // (4 * groups))
    cap_far = max(2, (5 * leaf_dev * far_dev + 4 * groups - 1) // (4 * groups))
    partial_value = jnp.einsum(
        "lrp,lsp->lrs", charges, projection, preferred_element_type=jnp.float32
    ).astype(jnp.bfloat16)
    skeleton_charges = lax.all_gather(partial_value, "nbr", axis=2, tiled=True)
    skeleton_points = jnp.take_along_axis(points, skeleton_index[:, None, :], axis=2)
    near_local, near_slots = slot_plan(near_ids, cap_near, groups, leaf_dev)
    far_local, far_slots = slot_plan(far_ids, cap_far, groups, leaf_dev)
    near_table = slot_table(near_local, near_slots, cap_near, groups)
    far_table = slot_table(far_local, far_slots, cap_far, groups)
    near_wanted, far_wanted = (
        lax.all_to_all(near_table, "leaf", split_axis=0, concat_axis=0, tiled=True),
        lax.all_to_all(far_table, "leaf", split_axis=0, concat_axis=0, tiled=True),
    )
    near_points, near_weights, far_points, far_weights = (
        lax.all_to_all(points[near_wanted], "leaf", split_axis=0, concat_axis=0, tiled=True),
        lax.all_to_all(charges[near_wanted], "leaf", split_axis=0, concat_axis=0, tiled=True),
        lax.all_to_all(
            skeleton_points[far_wanted], "leaf", split_axis=0, concat_axis=0, tiled=True
        ),
        lax.all_to_all(
            skeleton_charges[far_wanted], "leaf", split_axis=0, concat_axis=0, tiled=True
        ),
    )
    sources = jnp.concatenate(
        [
            gather_entries(near_points, near_slots, leaf_dev),
            gather_entries(far_points, far_slots, leaf_dev),
        ],
        axis=2,
    )
    weights = jnp.concatenate(
        [
            gather_entries(near_weights, near_slots, leaf_dev),
            gather_entries(far_weights, far_slots, leaf_dev),
        ],
        axis=2,
    )
    terms = group_terms(points, sources, weights)
    return lax.psum_scatter(terms, "nbr", scatter_dimension=2, tiled=True)


def solution(mesh):
    in_specs = (
        P("leaf", None, None),
        P("leaf", None, None),
        P("leaf", "nbr", None),
        P("leaf", None),
        P("leaf", "nbr"),
        P("leaf", "nbr"),
    )
    out_specs = P("leaf", None, "nbr")
    return jax.shard_map(
        per_device, mesh=mesh, in_specs=in_specs, out_specs=out_specs, check_vma=False
    )
```

profile of v0, /device:TPU:0, one launch (start us, length us, event | category | flops | bytes accessed | tf_op | source)
XLA Modules:
  0.0 668.9 jit_solution(7180529218226698054)
XLA Ops:
  23.7 132.5 %gather_fusion.8 = bf16[8192,32]{1,0:T(8,128)(2,1)} fusion(bf16[32,32,512]{1,2,0:T(8,128)(2,1)} %copy.77, s32[8192]{0:T(1024)S(1)} %bitcast.83), kind=kCustom, calls=%fused_computation.8 | custom fusion | bytes 1114112 | tf_op jit(solution)/shard_map/jit(take_along_axis)/gather | solution.py:84
  168.8 9.2 %gather_fusion.6 = bf16[160,32,256]{1,2,0:T(8,128)(2,1)} fusion(bf16[32,32,256]{1,2,0:T(8,128)(2,1)} %select_bitcast_fusion, s32[1024]{0:T(1024)S(1)} %pad_clamp_fusion.1), kind=kCustom, calls=%fused_computation.6 | custom fusion | bytes 5243520 | tf_op jit(solution)/shard_map/gather | solution.py:97
  178.0 9.8 %copy.78 = bf16[32,5,32,256]{3,2,1,0:T(8,128)(2,1)} copy(bf16[32,5,32,256]{2,3,1,0:T(8,128)(2,1)} %bitcast.89) | data formatting | bytes 5242880 | tf_op jit(solution)/shard_map/gather | solution.py:97
  198.3 31.7 %all-to-all-done.5 = bf16[32,5,32,256]{3,2,1,0:T(8,128)(2,1)} async-done(((bf16[32,5,32,256]{3,2,1,0:T(8,128)(2,1)}), bf16[32,5,32,256]{3,2,1,0:T(8,128)(2,1)}, u32[]{:S(2)}, u32[]{:S(2)}) %all-to-all-start.5) | async-done | bytes 2621472 | tf_op jit(solution)/shard_map/all_to_all | solution.py:96
  240.8 34.2 %all-to-all-done.4 = bf16[32,3,32,512]{3,2,1,0:T(8,128)(2,1)} async-done(((bf16[32,3,32,512]{3,2,1,0:T(8,128)(2,1)}), bf16[32,3,32,512]{3,2,1,0:T(8,128)(2,1)}, u32[]{:S(2)}, u32[]{:S(2)}) %all-to-all-start.4) | async-done | bytes 3145760 | tf_op jit(solution)/shard_map/all_to_all | solution.py:94
  279.9 11.4 %all-gather.2.cloned.1.call-start = ((), (), s32[]{:S(2)}) async-start(), calls=%async_computation.7 | async-start | bytes 2621440 | tf_op jit(solution)/shard_map/all_gather | solution.py:83
  296.9 33.5 %all-gather.2.cloned.1.call-done = bf16[32,64,256]{1,0,2:T(8,128)(2,1)} async-done(((bf16[32,64,64]{1,0,2:T(8,128)(2,1)}), bf16[32,64,256]{1,0,2:T(8,128)(2,1)}) %all-gather.2.cloned.1.call-update) | async-done | bytes 1048592 | tf_op jit(solution)/shard_map/all_gather | solution.py:83
  340.9 18.8 %all-to-all-done.1 = bf16[32,3,64,512]{3,2,1,0:T(8,128)(2,1)} async-done(((bf16[32,3,64,512]{3,2,1,0:T(8,128)(2,1)}), bf16[32,3,64,512]{3,2,1,0:T(8,128)(2,1)}, u32[]{:S(2)}, u32[]{:S(2)}) %all-to-all-start.1) | async-done | bytes 6291488 | tf_op jit(solution)/shard_map/all_to_all | solution.py:95
  359.8 11.3 %all-to-all-start.3 = ((bf16[32,5,64,256]{3,2,1,0:T(8,128)(2,1)}), bf16[32,5,64,256]{3,2,1,0:T(8,128)(2,1)}, u32[]{:S(2)}, u32[]{:S(2)}) async-start(bf16[32,5,64,256]{3,2,1,0:T(8,128)(2,1)} %bitcast.86), calls=%async_computation.3 | async-start | bytes 10485760 | tf_op jit(solution)/shard_map/all_to_all | solution.py:99
  402.2 8.5 %copy.69 = bf16[32,64,2,512]{3,2,1,0:T(2,128)(2,1)} copy(bf16[32,64,2,512]{3,1,2,0:T(8,128)(2,1)} %bitcast.87) | data formatting | bytes 8388608 | tf_op jit(solution)/shard_map/transpose | solution.py:68
  418.4 17.8 %all-to-all-done.3 = bf16[32,5,64,256]{3,2,1,0:T(8,128)(2,1)} async-done(((bf16[32,5,64,256]{3,2,1,0:T(8,128)(2,1)}), bf16[32,5,64,256]{3,2,1,0:T(8,128)(2,1)}, u32[]{:S(2)}, u32[]{:S(2)}) %all-to-all-start.3) | async-done | bytes 5242912 | tf_op jit(solution)/shard_map/all_to_all | solution.py:99
  441.4 8.1 %copy.75 = bf16[32,64,4,256]{3,2,1,0:T(4,128)(2,1)} copy(bf16[32,64,4,256]{3,1,2,0:T(8,128)(2,1)} %bitcast.88) | data formatting | bytes 8388608 | tf_op jit(solution)/shard_map/transpose | solution.py:68
  449.5 7.8 %concatenate.17 = bf16[8,4,64,1024]{3,2,1,0:T(8,128)(2,1)} reshape(bf16[32,64,4,256]{3,2,1,0:T(4,128)(2,1)} %copy.75) | data formatting | bytes 8388608 | tf_op jit(solution)/shard_map/concatenate | solution.py:110
  457.3 8.2 %pad_maximum_fusion = bf16[8,4,64,2048]{3,2,1,0:T(8,128)(2,1)} fusion(bf16[8,4,64,1024]{3,2,1,0:T(8,128)(2,1)} %concatenate.17, bf16[8,4,64,1024]{3,2,1,0:T(8,128)(2,1)} %concatenate.16), kind=kLoop, calls=%fused_computation.34 | loop fusion | flops 16777216 | bytes 16777216 | tf_op jit(solution)/shard_map/concatenate | solution.py:110
  465.5 146.8 %while.10 = (s32[]{:T(128)}, f32[8,4,64,512]{3,2,1,0:T(8,128)}, bf16[8,4,64,2048]{3,2,1,0:T(8,128)(2,1)}, bf16[8,4,32,512]{3,2,1,0:T(8,128)(2,1)S(1)}, bf16[8,4,32,2048]{3,2,1,0:T(8,128)(2,1)}, /*index=5*/s32[]{:T(128)}) while((s32[]{:T(128)}, f32[8,4,64,512]{3,2,1,0:T(8,128)}, bf16[8,4,64,2048]{3,2,1,0:T(8,128)(2,1)}, ...), condition=%wide.region_9.10_spmd, body=%wide.region_6.9_spmd.sunk | while | flops 3507410944 | bytes 36522060 | solution.py:44
  470.4 13.6 %fusion.45 = f32[8,4,64,512]{3,2,1,0:T(8,128)} fusion(f32[8,4,64,512]{3,2,1,0:T(8,128)} %get-tuple-element.85, s32[]{:T(128)} %get-tuple-element.84, f32[4,512,2048]{2,1,0:T(8,128)S(1)} %fusion.44, f32[4,2048]{1,0:T(4,128)S(1)} %multiply_reduce_fusion.4, f32[4,512]{1,0:T(4,128)S(1)} %multiply_reduce_fusion.5, ...), kind=kOutput, calls=%fused_computation.20.clone.1 | convolution fusion | flops 3238002688 | bytes 18392064 | tf_op jit(solution)/shard_map/while/body/eval_jaxpr/vmap(rm,tm->rt)/dot_general | solution.py:21
  488.7 13.6 %fusion.45 = f32[8,4,64,512]{3,2,1,0:T(8,128)} fusion(f32[8,4,64,512]{3,2,1,0:T(8,128)} %get-tuple-element.85, s32[]{:T(128)} %get-tuple-element.84, f32[4,512,2048]{2,1,0:T(8,128)S(1)} %fusion.44, f32[4,2048]{1,0:T(4,128)S(1)} %multiply_reduce_fusion.4, f32[4,512]{1,0:T(4,128)S(1)} %multiply_reduce_fusion.5, ...), kind=kOutput, calls=%fused_computation.20.clone.1 | convolution fusion | flops 3238002688 | bytes 18392064 | tf_op jit(solution)/shard_map/while/body/eval_jaxpr/vmap(rm,tm->rt)/dot_general | solution.py:21
  507.0 13.6 %fusion.45 = f32[8,4,64,512]{3,2,1,0:T(8,128)} fusion(f32[8,4,64,512]{3,2,1,0:T(8,128)} %get-tuple-element.85, s32[]{:T(128)} %get-tuple-element.84, f32[4,512,2048]{2,1,0:T(8,128)S(1)} %fusion.44, f32[4,2048]{1,0:T(4,128)S(1)} %multiply_reduce_fusion.4, f32[4,512]{1,0:T(4,128)S(1)} %multiply_reduce_fusion.5, ...), kind=kOutput, calls=%fused_computation.20.clone.1 | convolution fusion | flops 3238002688 | bytes 18392064 | tf_op jit(solution)/shard_map/while/body/eval_jaxpr/vmap(rm,tm->rt)/dot_general | solution.py:21
  525.4 13.6 %fusion.45 = f32[8,4,64,512]{3,2,1,0:T(8,128)} fusion(f32[8,4,64,512]{3,2,1,0:T(8,128)} %get-tuple-element.85, s32[]{:T(128)} %get-tuple-element.84, f32[4,512,2048]{2,1,0:T(8,128)S(1)} %fusion.44, f32[4,2048]{1,0:T(4,128)S(1)} %multiply_reduce_fusion.4, f32[4,512]{1,0:T(4,128)S(1)} %multiply_reduce_fusion.5, ...), kind=kOutput, calls=%fused_computation.20.clone.1 | convolution fusion | flops 3238002688 | bytes 18392064 | tf_op jit(solution)/shard_map/while/body/eval_jaxpr/vmap(rm,tm->rt)/dot_general | solution.py:21
  543.7 13.6 %fusion.45 = f32[8,4,64,512]{3,2,1,0:T(8,128)} fusion(f32[8,4,64,512]{3,2,1,0:T(8,128)} %get-tuple-element.85, s32[]{:T(128)} %get-tuple-element.84, f32[4,512,2048]{2,1,0:T(8,128)S(1)} %fusion.44, f32[4,2048]{1,0:T(4,128)S(1)} %multiply_reduce_fusion.4, f32[4,512]{1,0:T(4,128)S(1)} %multiply_reduce_fusion.5, ...), kind=kOutput, calls=%fused_computation.20.clone.1 | convolution fusion | flops 3238002688 | bytes 18392064 | tf_op jit(solution)/shard_map/while/body/eval_jaxpr/vmap(rm,tm->rt)/dot_general | solution.py:21
  562.0 13.6 %fusion.45 = f32[8,4,64,512]{3,2,1,0:T(8,128)} fusion(f32[8,4,64,512]{3,2,1,0:T(8,128)} %get-tuple-element.85, s32[]{:T(128)} %get-tuple-element.84, f32[4,512,2048]{2,1,0:T(8,128)S(1)} %fusion.44, f32[4,2048]{1,0:T(4,128)S(1)} %multiply_reduce_fusion.4, f32[4,512]{1,0:T(4,128)S(1)} %multiply_reduce_fusion.5, ...), kind=kOutput, calls=%fused_computation.20.clone.1 | convolution fusion | flops 3238002688 | bytes 18392064 | tf_op jit(solution)/shard_map/while/body/eval_jaxpr/vmap(rm,tm->rt)/dot_general | solution.py:21
  580.3 13.6 %fusion.45 = f32[8,4,64,512]{3,2,1,0:T(8,128)} fusion(f32[8,4,64,512]{3,2,1,0:T(8,128)} %get-tuple-element.85, s32[]{:T(128)} %get-tuple-element.84, f32[4,512,2048]{2,1,0:T(8,128)S(1)} %fusion.44, f32[4,2048]{1,0:T(4,128)S(1)} %multiply_reduce_fusion.4, f32[4,512]{1,0:T(4,128)S(1)} %multiply_reduce_fusion.5, ...), kind=kOutput, calls=%fused_computation.20.clone.1 | convolution fusion | flops 3238002688 | bytes 18392064 | tf_op jit(solution)/shard_map/while/body/eval_jaxpr/vmap(rm,tm->rt)/dot_general | solution.py:21
  598.6 13.6 %fusion.45 = f32[8,4,64,512]{3,2,1,0:T(8,128)} fusion(f32[8,4,64,512]{3,2,1,0:T(8,128)} %get-tuple-element.85, s32[]{:T(128)} %get-tuple-element.84, f32[4,512,2048]{2,1,0:T(8,128)S(1)} %fusion.44, f32[4,2048]{1,0:T(4,128)S(1)} %multiply_reduce_fusion.4, f32[4,512]{1,0:T(4,128)S(1)} %multiply_reduce_fusion.5, ...), kind=kOutput, calls=%fused_computation.20.clone.1 | convolution fusion | flops 3238002688 | bytes 18392064 | tf_op jit(solution)/shard_map/while/body/eval_jaxpr/vmap(rm,tm->rt)/dot_general | solution.py:21
  612.3 49.3 %reduce-scatter.2.cloned.1.call-done = f32[32,64,128]{2,1,0:T(8,128)} async-done(((f32[32,64,512]{2,1,0:T(8,128)}), f32[32,64,128]{2,1,0:T(8,128)}) %reduce-scatter.2.cloned.1.call-update) | async-done | bytes 1048592 | tf_op jit(solution)/shard_map/reduce_scatter | solution.py:118
  (96 shorter events, 153.4 us)
Async XLA Ops:
  6.5 228.3 %copy-start = (bf16[32,64,512]{2,1,0:T(8,128)(2,1)S(1)}, bf16[32,64,512]{2,1,0:T(8,128)(2,1)}, u32[]{:S(2)}) copy-start(bf16[32,64,512]{2,1,0:T(8,128)(2,1)} %param.9) | copy-start | bytes 6291460
  8.9 152.6 %all-to-all-start.2 = ((s32[32,1,5]{2,1,0:T(1,128)}), s32[32,1,5]{2,1,0:T(1,128)S(1)}, u32[]{:S(2)}, u32[]{:S(2)}) async-start(s32[32,1,5]{2,1,0:T(1,128)} %bitcast.12), calls=%async_computation.2 | async-start | bytes 32768 | tf_op jit(solution)/shard_map/all_to_all | solution.py:91
  161.5 26.3 %all-to-all-start = ((s32[32,1,3]{2,1,0:T(1,128)}), s32[32,1,3]{2,1,0:T(1,128)S(1)}, u32[]{:S(2)}, u32[]{:S(2)}) async-start(s32[32,1,3]{2,1,0:T(1,128)} %bitcast.4), calls=%async_computation | async-start | bytes 32768 | tf_op jit(solution)/shard_map/all_to_all | solution.py:90
  187.7 7.9 %copy-start.2 = (bf16[32,32,512]{2,1,0:T(8,128)(2,1)S(1)}, bf16[32,32,512]{2,1,0:T(8,128)(2,1)}, u32[]{:S(2)}) copy-start(bf16[32,32,512]{2,1,0:T(8,128)(2,1)} %param.8) | copy-start | bytes 3145732
  187.8 42.2 %all-to-all-start.5 = ((bf16[32,5,32,256]{3,2,1,0:T(8,128)(2,1)}), bf16[32,5,32,256]{3,2,1,0:T(8,128)(2,1)}, u32[]{:S(2)}, u32[]{:S(2)}) async-start(bf16[32,5,32,256]{3,2,1,0:T(8,128)(2,1)} %copy.78), calls=%async_computation.5 | async-start | bytes 5242880 | tf_op jit(solution)/shard_map/all_to_all | solution.py:96
  230.0 45.0 %all-to-all-start.4 = ((bf16[32,3,32,512]{3,2,1,0:T(8,128)(2,1)}), bf16[32,3,32,512]{3,2,1,0:T(8,128)(2,1)}, u32[]{:S(2)}, u32[]{:S(2)}) async-start(bf16[32,3,32,512]{3,2,1,0:T(8,128)(2,1)} %bitcast.90), calls=%async_computation.4 | async-start | bytes 6291456 | tf_op jit(solution)/shard_map/all_to_all | solution.py:94
  275.0 84.8 %all-to-all-start.1 = ((bf16[32,3,64,512]{3,2,1,0:T(8,128)(2,1)}), bf16[32,3,64,512]{3,2,1,0:T(8,128)(2,1)}, u32[]{:S(2)}, u32[]{:S(2)}) async-start(bf16[32,3,64,512]{3,2,1,0:T(8,128)(2,1)} %bitcast.85), calls=%async_computation.1 | async-start | bytes 12582912 | tf_op jit(solution)/shard_map/all_to_all | solution.py:95
  279.9 50.6 %all-gather.2.cloned.1.call-start = ((), (), s32[]{:S(2)}) async-start(), calls=%async_computation.7 | async-start | bytes 2621440 | tf_op jit(solution)/shard_map/all_gather | solution.py:83
  359.8 76.4 %all-to-all-start.3 = ((bf16[32,5,64,256]{3,2,1,0:T(8,128)(2,1)}), bf16[32,5,64,256]{3,2,1,0:T(8,128)(2,1)}, u32[]{:S(2)}, u32[]{:S(2)}) async-start(bf16[32,5,64,256]{3,2,1,0:T(8,128)(2,1)} %bitcast.86), calls=%async_computation.3 | async-start | bytes 10485760 | tf_op jit(solution)/shard_map/all_to_all | solution.py:99
  371.1 290.5 %reduce-scatter.2.cloned.1.call-start = ((), (), s32[]{:S(2)}) async-start(), calls=%async_computation.8 | async-start | bytes 5242880 | tf_op jit(solution)/shard_map/reduce_scatter | solution.py:118
  387.8 4.6 copy-start.3
  612.3 49.3 %copy-start.1 = (bf16[32,64,512]{2,1,0:T(8,128)(2,1)S(1)}, bf16[32,64,512]{2,1,0:T(8,128)(2,1)}, u32[]{:S(2)}) copy-start(bf16[32,64,512]{2,1,0:T(8,128)(2,1)} %param.9) | copy-start | bytes 6291460
Sparse Core Ops, SparseCore 0:
  297.0 33.3 all-gather.1
  612.4 49.0 reduce-scatter.1
where the time goes:
time: 679 us; the launch traced here: 669 us
  local copies, waits for them, and re-layouts  246 us (36%)
  waiting for transfers between devices  185 us (27%)
  matrix products  139 us (20%)
  starting transfers between devices  54.7 us (8%)
  other arithmetic  29.4 us (4%)
  between operations  14.1 us (2%)
    gather x1, local copies, waits for them, and re-layouts, per_device(): jnp.take_along_axis(points, skeleton_index[:, None, :], axis=2)  133 us
    dot_general x8, matrix products, kernel_terms(): jnp.einsum('rm,tm->rt', weights.astype(jnp.float32), kernel, precision=la...  109 us
    reduce_scatter x1, waiting for transfers between devices, per_device(): return lax.psum_scatter(terms, 'nbr', scatter_dimension=2, tiled=True)  49.3 us
    all_to_all x1, waiting for transfers between devices, per_device(): lax.all_to_all(points[near_wanted], 'leaf', split_axis=0, concat_axis=0,...  34.2 us
    all_gather x1, waiting for transfers between devices, per_device(): skeleton_charges = lax.all_gather(partial_value, 'nbr', axis=2, tiled=True)  33.5 us
    all_to_all x1, waiting for transfers between devices, per_device(): lax.all_to_all(skeleton_points[far_wanted], 'leaf', split_axis=0, concat_...  31.7 us
    dot_general x8, matrix products, kernel_terms(): jnp.einsum('dt,dm->tm', targets, sources, preferred_element_type=jnp.floa...  27.3 us
    transpose x4, local copies, waits for them, and re-layouts, gather_entries(): picked.transpose(0, 2, 1, 3)  23.5 us
  transfers between devices with their start and end apart: 8, of which 6 were waited for; matrix products, arithmetic and copies ran while one was open for 35% of the time, Pallas kernels for 0%

commit v1 on v0

v1 whole, which is shorter than its diff:
```python
import functools
import math

import jax
import jax.numpy as jnp
from jax import lax
from jax.experimental import pallas as pl
from jax.experimental.pallas import tpu as pltpu
from jax.sharding import PartitionSpec as P

MESH = pl.DeviceIdType.MESH
ANY = pl.BlockSpec(memory_space=pl.ANY)
VMEM = pl.BlockSpec(memory_space=pltpu.VMEM)
SMEM = pl.BlockSpec(memory_space=pltpu.SMEM)
RING = 4
NEAR_SLOTS = 6
FAR_SLOTS = 10
LIMIT = 62 * 1024 * 1000
F32 = jnp.float32
BF16 = jnp.bfloat16


def torus_position():
    leaf = lax.axis_index("leaf")
    chip = leaf // 2
    return chip // RING, chip % RING, leaf % 2, lax.axis_index("nbr")


def wrap(value):
    return lax.rem(value + 2 * RING, RING)


def pick(first_is_x, u, v):
    return u * RING + v if first_is_x else v * RING + u


def quarter_kernel(charges, projection, out):
    half = charges.shape[0] // 2

    def body(leaf, carry):
        parts = []
        for item in (leaf, leaf + half):
            parts.append(
                lax.dot_general(
                    charges[item], projection[item], (((1,), (1,)), ((), ())), preferred_element_type=F32
                )
            )
        out[leaf] = jnp.concatenate(parts, axis=1).astype(BF16)
        return carry

    lax.fori_loop(0, half, body, 0, unroll=2)


def gather_kernel(
    points, charges, quarter, index, ids,
    x_all, points_sib, charges_sib, index_sib, quarter_own, quarter_sib, ids_all,
    send_x, recv_x, send_s, recv_s, send_i, recv_i, local_sem,
):
    x, y, core, z = torus_position()
    n_z = quarter_own.shape[0]
    leaf_dev, dim, _ = points.shape
    cols = x_all.shape[3]
    half, part = leaf_dev // 2, leaf_dev // 4
    me = (x * RING + y) * n_z + z
    n_ids = ids_all.shape[0]

    def device(chip, core_at, z_at):
        return (chip * 2 + core_at, z_at)

    own_ids = pltpu.make_async_copy(ids, ids_all.at[me], local_sem)
    own_ids.start()

    def send_ids(step, carry):
        peer = lax.rem(me + step, n_ids)
        pltpu.make_async_remote_copy(
            src_ref=ids, dst_ref=ids_all.at[me], send_sem=send_i, recv_sem=recv_i,
            device_id=device(peer // n_z, core, lax.rem(peer, n_z)), device_id_type=MESH,
        ).start()
        return carry

    lax.fori_loop(1, n_ids, send_ids, 0)

    sends = []

    def message(kind, sems, src, dst, target):
        copy = pltpu.make_async_remote_copy(
            src_ref=src, dst_ref=dst, send_sem=sems[0].at[kind], recv_sem=sems[1].at[kind],
            device_id=target, device_id_type=MESH,
        )
        return copy

    def start(copy):
        copy.start()
        sends.append(copy)

    here = x * RING + y
    side = (send_s, recv_s)
    line = (send_x, recv_x)

    own_x = []
    for half_at in range(2):
        first_x = half_at == 0
        u, v = (x, y) if first_x else (y, x)
        base = half_at * half
        rows = pl.ds(base, half)
        src = points.at[rows, :, pl.ds(pl.multiple_of(z * cols, cols), cols)]
        dst = x_all.at[here, rows]
        kinds = 20 * half_at
        own_x.append(
            [
                message(kinds + 0, line, src, dst, device(pick(first_x, wrap(u + 1), v), core, z)),
                message(kinds + 1, line, src, dst, device(pick(first_x, wrap(u - 1), v), core, z)),
                message(kinds + 4, line, src, dst, device(pick(first_x, u, wrap(v + 1)), core, z)),
                message(kinds + 5, line, src, dst, device(pick(first_x, u, wrap(v - 1)), core, z)),
            ]
        )
    for at in range(4):
        for half_at in range(2):
            start(own_x[half_at][at])

    z_copies = []
    for step in range(1, n_z):
        copy = message(step, side, quarter, quarter_own.at[z], device(here, core, lax.rem(z + step, n_z)))
        start(copy)
        z_copies.append(copy)
    sib_copies = []
    for at, (src, dst) in enumerate(((points, points_sib), (charges, charges_sib), (index, index_sib))):
        copy = message(8 + at, side, src, dst, device(here, 1 - core, z))
        start(copy)
        sib_copies.append(copy)
    copy = message(0, side, quarter, quarter_sib.at[z], device(here, 1 - core, z))
    start(copy)
    sib_copies.append(copy)

    def item(half_at, du, dv, quarter_at=None):
        first_x = half_at == 0
        u, v = (x, y) if first_x else (y, x)
        rows = pl.ds(half_at * half, half) if quarter_at is None else pl.ds(half_at * half + quarter_at * part, part)
        return x_all.at[pick(first_x, wrap(u + du), wrap(v + dv)), rows]

    def target(half_at, du, dv):
        first_x = half_at == 0
        u, v = (x, y) if first_x else (y, x)
        return device(pick(first_x, wrap(u + du), wrap(v + dv)), core, z)

    def arrived(half_at, kind, ref):
        message(20 * half_at + kind, line, ref, ref, target(half_at, 1, 0)).wait_recv()

    def forward(half_at, kind, ref, du, dv):
        start(message(20 * half_at + kind, line, ref, ref, target(half_at, du, dv)))

    def across(half_at, slot, du):
        ref = item(half_at, du, 0)
        forward(half_at, 4 + 4 * slot, ref, 0, 1)
        forward(half_at, 5 + 4 * slot, ref, 0, -1)

    def relay(half_at, slot, du):
        arrived(half_at, 4 + 4 * slot, item(half_at, du, -1))
        forward(half_at, 6 + 4 * slot, item(half_at, du, -1, 0), 0, 1)
        arrived(half_at, 5 + 4 * slot, item(half_at, du, 1))
        forward(half_at, 7 + 4 * slot, item(half_at, du, 1, 1), 0, -1)

    for half_at in range(2):
        arrived(half_at, 0, item(half_at, -1, 0))
        forward(half_at, 2, item(half_at, -1, 0, 0), 1, 0)
        across(half_at, 1, -1)
    for half_at in range(2):
        arrived(half_at, 1, item(half_at, 1, 0))
        forward(half_at, 3, item(half_at, 1, 0, 1), -1, 0)
        across(half_at, 2, 1)
    for half_at in range(2):
        relay(half_at, 0, 0)
    for step in range(1, n_z):
        z_copies[step - 1].wait_recv()
        slot = lax.rem(z - step + n_z, n_z)
        ref = quarter_own.at[slot]
        copy = message(4 + step, side, ref, quarter_sib.at[slot], device(here, 1 - core, z))
        start(copy)
        sib_copies.append(copy)
    for half_at in range(2):
        arrived(half_at, 2, item(half_at, 2, 0, 0))
        arrived(half_at, 3, item(half_at, 2, 0, 1))
        across(half_at, 3, 2)
    for slot, du in ((1, -1), (2, 1), (3, 2)):
        for half_at in range(2):
            relay(half_at, slot, du)
    for slot, du in ((0, 0), (1, -1), (2, 1), (3, 2)):
        for half_at in range(2):
            arrived(half_at, 6 + 4 * slot, item(half_at, du, 2, 0))
            arrived(half_at, 7 + 4 * slot, item(half_at, du, 2, 1))
    for copy in sib_copies:
        copy.wait_recv()
    for copy in sends:
        copy.wait_send()
    own_ids.wait()
    others = ids_all.at[pl.ds(0, n_ids - 1)]
    every = pltpu.make_async_remote_copy(
        src_ref=others, dst_ref=others, send_sem=send_i, recv_sem=recv_i,
        device_id=target(0, 1, 0), device_id_type=MESH,
    )
    every.wait_send()
    every.wait_recv()


def table_kernel(leaf_dev, near_dev, far_dev, n_z, ids_all, table):
    x, y, core, _ = torus_position()
    chip = x * RING + y
    rows = ids_all.shape[0]
    lane = lax.broadcasted_iota(jnp.int32, (rows, 128), 1)
    row = lax.broadcasted_iota(jnp.int32, (rows, 128), 0)
    upper = lax.broadcasted_iota(jnp.int32, (128, 128), 0) <= lax.broadcasted_iota(jnp.int32, (128, 128), 1)
    upper = jnp.where(upper, 1.0, 0.0).astype(BF16)
    result = jnp.zeros((rows, 128), jnp.int32)
    for at, (per_leaf, slots, start) in enumerate(((near_dev, NEAR_SLOTS, 0), (far_dev, FAR_SLOTS, NEAR_SLOTS))):
        ids = ids_all[:, at, :]
        named = lax.div(ids, 2 * leaf_dev)
        member = jnp.logical_and(named == chip, ids >= 0)
        source = lax.rem(lax.rem(ids, 2 * leaf_dev) + core * leaf_dev, 2 * leaf_dev)
        code = (lax.div(row, n_z) * leaf_dev + lax.div(lane, per_leaf)) * (2 * leaf_dev) + source
        flags = jnp.where(member, 1.0, 0.0)
        upto = jnp.dot(flags.astype(BF16), upper, preferred_element_type=F32).astype(jnp.int32)
        for slot in range(slots):
            chosen = jnp.logical_and(member, upto == slot + 1)
            value = jnp.sum(jnp.where(chosen, code, 0), axis=1, keepdims=True)
            result = jnp.where(lane == start + slot, value, result)
        count = jnp.sum(jnp.where(member, 1, 0), axis=1, keepdims=True)
        result = jnp.where(lane == NEAR_SLOTS + FAR_SLOTS + at, count, result)
    table[...] = result


def norm_rows(coords, sign_first):
    values = coords.astype(F32)
    norm = -jnp.sum(values * values, axis=0, keepdims=True)
    high = norm.astype(BF16).astype(F32)
    rest = norm - high
    middle = rest.astype(BF16).astype(F32)
    low = rest - middle
    shape = (16, coords.shape[1])
    row = lax.broadcasted_iota(jnp.int32, shape, 0)
    start = 0 if sign_first else 3
    ones = 3 if sign_first else 0
    result = jnp.where(jnp.logical_and(row >= ones, row < ones + 3), 1.0, 0.0)
    for at, piece in enumerate((high, middle, low)):
        result = jnp.where(row == start + at, jnp.broadcast_to(piece, shape), result)
    return result.astype(BF16)


def pair_kernel(
    table, x_all, points, charges, quarter, index, points_sib, charges_sib, index_sib, quarter_own, quarter_sib,
    out,
    x_raw, x_aug, y_table, w_table, p_buf, i_buf, q_buf, acc, s_a, s_b, items, sems,
):
    x, y, core, z = torus_position()
    chips, leaf_dev, dim, cols = x_all.shape
    leaf = points.shape[2]
    skel = index.shape[1]
    n_z = quarter_own.shape[0]
    here = x * RING + y
    sources = 2 * leaf_dev
    targets = chips * leaf_dev
    hold = leaf_dev // 2
    piece = skel // n_z

    loads = []

    def load(at, src, dst):
        copy = pltpu.make_async_copy(src, dst, sems.at[at])
        copy.start()
        loads.append(copy)

    load(0, points, p_buf.at[0])
    load(1, points_sib, p_buf.at[1])
    load(2, index, i_buf.at[0])
    load(3, index_sib, i_buf.at[1])
    load(4, quarter_own, q_buf.at[0])
    load(5, quarter_sib, q_buf.at[1])
    load(6, x_all, x_raw)
    at = 8
    for side, ref in ((0, charges), (1, charges_sib)):
        for half in range(2):
            load(
                at, ref.at[:, :, pl.ds(half * skel, skel)],
                w_table.at[pl.ds(half * sources + side * leaf_dev, leaf_dev)],
            )
            at += 1

    rows = table.shape[0]
    span = 3 * sources

    def fill(row, count):
        for slot in range(NEAR_SLOTS):
            code = table[row, slot]
            base = lax.div(code, sources) * 256 + lax.rem(code, sources)
            items[count + 2 * slot] = base
            items[count + 2 * slot + 1] = base + sources
        count = count + 2 * table[row, NEAR_SLOTS + FAR_SLOTS]
        for slot in range(FAR_SLOTS):
            code = table[row, NEAR_SLOTS + slot]
            items[count + slot] = lax.div(code, sources) * 256 + lax.rem(code, sources) + 2 * sources
        return count + table[row, NEAR_SLOTS + FAR_SLOTS + 1]

    count = lax.fori_loop(0, rows, fill, 0)
    for at in range(12):
        items[count + at] = targets * 256

    for copy in loads:
        copy.wait()
    copy = pltpu.make_async_copy(quarter, q_buf.at[0, z], sems.at[7])
    copy.start()
    own = pltpu.make_async_copy(
        points.at[:, :, pl.ds(pl.multiple_of(z * cols, cols), cols)], x_raw.at[here], sems.at[6]
    )
    own.start()

    def zero(at, carry):
        acc[at] = jnp.zeros(acc.shape[1:], F32)
        return carry

    lax.fori_loop(0, targets + 1, zero, 0, unroll=4)
    copy.wait()
    own.wait()

    pad = jnp.zeros((16, cols), BF16)

    def widen(at, carry):
        coords = x_raw[lax.div(at, leaf_dev), lax.rem(at, leaf_dev)]
        x_aug[at] = jnp.concatenate([coords, norm_rows(coords, True), pad], axis=0)
        return carry

    lax.fori_loop(0, targets, widen, 0, unroll=4)

    wide_pad = jnp.zeros((16, leaf), BF16)
    point_number = lax.broadcasted_iota(jnp.int32, (leaf, skel), 0)

    def source(at, carry):
        side, item = lax.div(at, leaf_dev), lax.rem(at, leaf_dev)
        coords = p_buf[side, item]
        block = jnp.concatenate([coords + coords, norm_rows(coords, False), wide_pad], axis=0)
        block = jnp.concatenate([block, block], axis=0)
        turned = block.T
        y_table[at] = turned[:skel]
        y_table[sources + at] = turned[skel:]
        chosen = point_number == i_buf[side, pl.ds(item, 1), :]
        chosen = jnp.where(chosen, 1.0, 0.0).astype(BF16)
        picked = jnp.dot(block, chosen, preferred_element_type=F32).astype(BF16)
        y_table[2 * sources + at] = picked.T
        return carry

    lax.fori_loop(0, sources, source, 0, unroll=2)

    def assemble(at, carry):
        side, item = lax.div(at, hold), lax.rem(at, hold)
        chunks = [q_buf[side, step, item] for step in range(n_z)]
        for half in range(2):
            pieces = [chunk[:, half * piece : (half + 1) * piece] for chunk in chunks]
            w_table[2 * sources + side * leaf_dev + half * hold + item] = jnp.concatenate(pieces, axis=1)
        return carry

    lax.fori_loop(0, 2 * hold, assemble, 0, unroll=2)

    empty = jnp.zeros((64, cols), BF16)
    low_lanes = lax.broadcasted_iota(jnp.int32, (skel, 128), 1) < 64

    def read(at):
        code = items[at]
        return lax.div(code, 256), lax.rem(code, 256)

    def scores(group, buf):
        for duo in range(2):
            t_0, u_0 = read(group * 4 + 2 * duo)
            t_1, u_1 = read(group * 4 + 2 * duo + 1)
            x_0 = x_aug[jnp.minimum(t_0, targets - 1)]
            x_1 = x_aug[jnp.minimum(t_1, targets - 1)]
            right = jnp.concatenate(
                [jnp.concatenate([x_0, empty], axis=0), jnp.concatenate([empty, x_1], axis=0)], axis=1
            )
            left = jnp.where(low_lanes, y_table[u_0], y_table[u_1])
            buf[duo] = jnp.dot(left, right, preferred_element_type=F32)

    def sums(group, buf):
        for duo in range(2):
            t_0, u_0 = read(group * 4 + 2 * duo)
            t_1, u_1 = read(group * 4 + 2 * duo + 1)
            kernel = jnp.exp(buf[duo]).astype(BF16)
            weights = jnp.concatenate([w_table[u_0], w_table[u_1]], axis=0)
            terms = jnp.dot(weights, kernel, preferred_element_type=F32)
            rhs = terms.shape[0] // 2
            acc[t_0] = acc[t_0] + terms[:rhs, :cols]
            acc[t_1] = acc[t_1] + terms[rhs:, cols:]

    scores(0, s_a)

    def step(at, carry):
        scores(2 * at + 1, s_b)
        sums(2 * at, s_a)
        scores(2 * at + 2, s_a)
        sums(2 * at + 1, s_b)
        return carry

    lax.fori_loop(0, lax.div(count + 7, 8), step, 0)
    done = pltpu.make_async_copy(acc.at[pl.ds(0, targets)], out, sems.at[0])
    done.start()
    done.wait()


def reduce_kernel(
    part_all, out, held, send_8, recv_8, send_16, recv_16, scale_s8, scale_r8, scale_s16, scale_r16,
    load_sems, sem_s8, sem_r8, sem_s16, sem_r16,
):
    x, y, core, z = torus_position()
    leaf_dev = part_all.shape[1]
    half, part = leaf_dev // 2, leaf_dev // 4
    order = ((2, 0), (1, 1), (-1, 2), (0, 3))

    def chip_at(half_at, du, dv):
        first_x = half_at == 0
        u, v = (x, y) if first_x else (y, x)
        return pick(first_x, wrap(u + du), wrap(v + dv))

    loads = {}
    for du, _ in order:
        for dv, _ in order:
            for half_at in range(2):
                slot = chip_at(half_at, du, dv)
                ref = pl.ds(half_at * half, half)
                copy = pltpu.make_async_copy(
                    part_all.at[slot, ref], held.at[slot, ref], load_sems.at[len(loads)]
                )
                copy.start()
                loads[half_at, du, dv] = copy

    sends = []

    def wires(size, kind, chip):
        big = size == half
        pairs = (
            ((send_16, recv_16, sem_s16, sem_r16, 0), (scale_s16, scale_r16, sem_s16, sem_r16, 1))
            if big
            else ((send_8, recv_8, sem_s8, sem_r8, 0), (scale_s8, scale_r8, sem_s8, sem_r8, 1))
        )
        return [
            pltpu.make_async_remote_copy(
                src_ref=src.at[kind], dst_ref=dst.at[kind], send_sem=s.at[2 * kind + at], recv_sem=r.at[2 * kind + at],
                device_id=(chip * 2 + core, z), device_id_type=MESH,
            )
            for src, dst, s, r, at in pairs
        ]

    def unpack(size, kind, row):
        data, scale = (recv_16, scale_r16) if size == half else (recv_8, scale_r8)
        return data[kind, row].astype(jnp.int32).astype(F32) * scale[kind, pl.ds(row, 1), :]

    def send(size, kind, chip, value_at):
        data, scale = (send_16, scale_s16) if size == half else (send_8, scale_s8)

        def body(row, carry):
            value = value_at(row)
            top = jnp.maximum(jnp.max(jnp.abs(value), axis=0, keepdims=True), 1e-30)
            scale[kind, pl.ds(row, 1), :] = top * (1.0 / 32767.0)
            data[kind, row] = jnp.round(value * (32767.0 / top)).astype(jnp.int32).astype(jnp.int16)
            return carry

        lax.fori_loop(0, size, body, 0, unroll=2)
        for copy in wires(size, kind, chip):
            copy.start()
            sends.append(copy)

    def wait(size, kind):
        for copy in wires(size, kind, chip_at(0, 1, 0)):
            copy.wait_recv()

    def ready(half_at, du, dv):
        loads.pop((half_at, du, dv)).wait()

    for dv, at in order:
        for half_at in range(2):
            base = half_at * half
            ready(half_at, 2, dv)
            slot = chip_at(half_at, 2, dv)
            kind = half_at * 10 + 2 * at
            send(part, kind, chip_at(half_at, 1, 0), lambda row: held[slot, base + row])
            send(part, kind + 1, chip_at(half_at, -1, 0), lambda row: held[slot, base + part + row])
    for dv, at in order:
        for half_at in range(2):
            base = half_at * half
            for du, side in ((1, 0), (-1, 1)):
                ready(half_at, du, dv)
                slot = chip_at(half_at, du, dv)
                kind = half_at * 10 + 2 * at + side
                wait(part, kind)

                def add(row, carry):
                    spot = base + side * part + row
                    held[slot, spot] = held[slot, spot] + unpack(part, kind, row)
                    return carry

                lax.fori_loop(0, part, add, 0, unroll=2)
                send(half, kind, chip_at(half_at, du, 0), lambda row: held[slot, base + row])
    for dv, at in order:
        for half_at in range(2):
            base = half_at * half
            ready(half_at, 0, dv)
            slot = chip_at(half_at, 0, dv)
            kind = half_at * 10 + 2 * at
            wait(half, kind)
            wait(half, kind + 1)

            def keep(row, carry):
                held[slot, base + row] = held[slot, base + row] + unpack(half, kind, row) + unpack(half, kind + 1, row)
                return carry

            lax.fori_loop(0, half, keep, 0, unroll=2)
            if dv == 2:
                for sign, side in ((1, 0), (-1, 1)):
                    send(
                        part, half_at * 10 + 8 + side, chip_at(half_at, 0, sign),
                        lambda row: held[slot, base + side * part + row],
                    )
            elif dv != 0:
                side = 0 if dv == 1 else 1
                late = half_at * 10 + 8 + side
                wait(part, late)

                def add_late(row, carry):
                    spot = base + side * part + row
                    held[slot, spot] = held[slot, spot] + unpack(part, late, row)
                    return carry

                lax.fori_loop(0, part, add_late, 0, unroll=2)
                send(half, late, chip_at(half_at, 0, dv), lambda row: held[slot, base + row])
    for half_at in range(2):
        base = half_at * half
        slot = chip_at(half_at, 0, 0)
        kind = half_at * 10 + 8
        wait(half, kind)
        wait(half, kind + 1)

        def finish(row, carry):
            out[base + row] = held[slot, base + row] + unpack(half, kind, row) + unpack(half, kind + 1, row)
            return carry

        lax.fori_loop(0, half, finish, 0, unroll=2)
    for copy in sends:
        copy.wait_send()


def per_device(points, charges, projection, skeleton_index, near_ids, far_ids):
    leaf_dev, dim, leaf = points.shape
    rhs = charges.shape[1]
    skel = skeleton_index.shape[1]
    n_z = lax.axis_size("nbr")
    chips = lax.axis_size("leaf") // 2
    cols = leaf // n_z
    near_dev, far_dev = near_ids.shape[1], far_ids.shape[1]
    sources, targets = 2 * leaf_dev, chips * leaf_dev
    params = functools.partial(pltpu.CompilerParams, vmem_limit_bytes=LIMIT)
    dma = pltpu.SemaphoreType.DMA
    shape = jax.ShapeDtypeStruct

    def row_of(ids):
        flat = ids.reshape(1, -1)
        return jnp.pad(flat, ((0, 0), (0, 128 - flat.shape[1])), constant_values=-1)

    ids = jnp.concatenate([row_of(near_ids), row_of(far_ids), jnp.full((6, 128), -1, jnp.int32)], axis=0)

    quarter = pl.pallas_call(
        quarter_kernel,
        out_shape=shape((leaf_dev // 2, rhs, 2 * skel // n_z), BF16),
        in_specs=[VMEM, VMEM],
        out_specs=VMEM,
        name="quarter",
        compiler_params=params(),
    )(charges, projection)
    x_all, points_sib, charges_sib, index_sib, quarter_own, quarter_sib, ids_all = pl.pallas_call(
        gather_kernel,
        out_shape=[
            shape((chips, leaf_dev, dim, cols), BF16),
            shape(points.shape, BF16),
            shape(charges.shape, BF16),
            shape(skeleton_index.shape, jnp.int32),
            shape((n_z,) + quarter.shape, BF16),
            shape((n_z,) + quarter.shape, BF16),
            shape((chips * n_z, 8, 128), jnp.int32),
        ],
        in_specs=[ANY] * 5,
        out_specs=[ANY] * 7,
        scratch_shapes=[dma((40,)), dma((40,)), dma((12,)), dma((12,)), dma, dma, dma],
        name="gather",
        compiler_params=params(has_side_effects=True),
    )(points, charges, quarter, skeleton_index, ids)
    table = pl.pallas_call(
        functools.partial(table_kernel, leaf_dev, near_dev, far_dev, n_z),
        out_shape=shape((chips * n_z, 128), jnp.int32),
        in_specs=[VMEM],
        out_specs=VMEM,
        name="table",
        compiler_params=params(),
    )(ids_all)
    partial_sums = pl.pallas_call(
        pair_kernel,
        out_shape=shape((targets, rhs, cols), F32),
        in_specs=[SMEM] + [ANY] * 10,
        out_specs=ANY,
        scratch_shapes=[
            pltpu.VMEM((chips, leaf_dev, dim, cols), BF16),
            pltpu.VMEM((targets, 64, cols), BF16),
            pltpu.VMEM((3 * sources, skel, 128), BF16),
            pltpu.VMEM((3 * sources, rhs, skel), BF16),
            pltpu.VMEM((2,) + points.shape, BF16),
            pltpu.VMEM((2,) + skeleton_index.shape, jnp.int32),
            pltpu.VMEM((2, n_z) + quarter.shape, BF16),
            pltpu.VMEM((targets + 1, rhs, cols), F32),
            pltpu.VMEM((2, skel, 2 * cols), F32),
            pltpu.VMEM((2, skel, 2 * cols), F32),
            pltpu.SMEM((chips * n_z * (2 * NEAR_SLOTS + FAR_SLOTS) + 32,), jnp.int32),
            dma((16,)),
        ],
        name="pairs",
        compiler_params=params(),
    )(
        table, x_all, points, charges, quarter, skeleton_index, points_sib, charges_sib, index_sib, quarter_own,
        quarter_sib,
    )
    half, part = leaf_dev // 2, leaf_dev // 4
    return pl.pallas_call(
        reduce_kernel,
        out_shape=shape((leaf_dev, rhs, cols), F32),
        in_specs=[ANY],
        out_specs=VMEM,
        scratch_shapes=[
            pltpu.VMEM((chips, leaf_dev, rhs, cols), F32),
            pltpu.VMEM((20, part, rhs, cols), jnp.int16),
            pltpu.VMEM((20, part, rhs, cols), jnp.int16),
            pltpu.VMEM((20, half, rhs, cols), jnp.int16),
            pltpu.VMEM((20, half, rhs, cols), jnp.int16),
            pltpu.VMEM((20, part, cols), F32),
            pltpu.VMEM((20, part, cols), F32),
            pltpu.VMEM((20, half, cols), F32),
            pltpu.VMEM((20, half, cols), F32),
            dma((32,)), dma((40,)), dma((40,)), dma((40,)), dma((40,)),
        ],
        name="reduce",
        compiler_params=params(has_side_effects=True),
    )(partial_sums.reshape(chips, leaf_dev, rhs, cols))


def solution(mesh):
    in_specs = (
        P("leaf", None, None),
        P("leaf", None, None),
        P("leaf", "nbr", None),
        P("leaf", None),
        P("leaf", "nbr"),
        P("leaf", "nbr"),
    )
    out_specs = P("leaf", None, "nbr")
    return jax.shard_map(per_device, mesh=mesh, in_specs=in_specs, out_specs=out_specs, check_vma=False)
```

time: 679 us -> 203 us (0.30); the launches traced: 669 us -> 203 us
  local copies, waits for them, and re-layouts: 246 us -> 4.12 us
  Pallas kernels: 0 us -> 198 us
  waiting for transfers between devices: 185 us -> 0 us
  matrix products: 139 us -> 0 us
  starting transfers between devices: 54.7 us -> 0 us
  other arithmetic: 29.4 us -> 0.67 us
  between operations: 14.1 us -> 0.03 us
    pallas_call x0 -> x5, Pallas kernels: none -> 198 us  [the longest x1 84.9 us: per_device(): pl.pallas_call(pair_kernel, out_shape=shape((targets, rhs, cols), F32), i...]
    gather x10 -> x0, local copies, waits for them, and re-layouts: 184 us -> none  [the longest x1 133 us: per_device(): jnp.take_along_axis(points, skeleton_index[:, None, :], axis=2)]
    dot_general x17 -> x0, matrix products: 139 us -> none  [the longest x8 109 us: kernel_terms(): jnp.einsum('rm,tm->rt', weights.astype(jnp.float32), kernel, precision=la...]
    all_to_all x6 -> x0, waiting for transfers between devices: 103 us -> none  [the longest x1 34.2 us: per_device(): lax.all_to_all(points[near_wanted], 'leaf', split_axis=0, concat_axis=0,...]
    reduce_scatter x1 -> x0, waiting for transfers between devices: 49.3 us -> none  [per_device(): return lax.psum_scatter(terms, 'nbr', scatter_dimension=2, tiled=True)]
    all_to_all x6 -> x0, starting transfers between devices: 43.3 us -> none  [the longest x1 11.3 us: per_device(): lax.all_to_all(skeleton_charges[far_wanted], 'leaf', split_axis=0, concat...]
    all_gather x1 -> x0, waiting for transfers between devices: 33.5 us -> none  [per_device(): skeleton_charges = lax.all_gather(partial_value, 'nbr', axis=2, tiled=True)]
    concatenate x4 -> x1, local copies, waits for them, and re-layouts: 24.6 us -> 0.08 us  [per_device(): jnp.concatenate([row_of(near_ids), row_of(far_ids), jnp.full((6, 128), -1...]
  transfers between devices with their start and end apart: 8 -> 0, of which waited for: 6 -> 0; matrix products, arithmetic and copies ran while one was open for 35% -> 0% of each run, Pallas kernels for 0% -> 0%
where the time goes in v1:
time: 203 us
  Pallas kernels  198 us (98%)
  local copies, waits for them, and re-layouts  4.12 us (2%)
    pallas_call x1, Pallas kernels, per_device(): pl.pallas_call(pair_kernel, out_shape=shape((targets, rhs, cols), F32), i...  84.9 us
    pallas_call x1, Pallas kernels, per_device(): pl.pallas_call(reduce_kernel, out_shape=shape((leaf_dev, rhs, cols), F32)...  61.8 us
    pallas_call x1, Pallas kernels, per_device(): pl.pallas_call(gather_kernel, out_shape=[shape((chips, leaf_dev, dim, col...  43.5 us
    pallas_call x1, Pallas kernels, per_device(): pl.pallas_call(quarter_kernel, out_shape=shape((leaf_dev // 2, rhs, 2 * s...  5.21 us

profile of v1, /device:TPU:0, one launch (start us, length us, event | category | flops | bytes accessed | tf_op | source)
XLA Modules:
  0.0 202.7 jit_solution(10726710581219442698)
XLA Ops:
  0.0 0.1 pad.7.clone
  0.1 0.8 copy.9
  0.8 0.1 reshape.9
  0.9 0.8 copy.10
  1.7 0.1 reshape.10
  1.8 0.7 fusion.ids
  2.5 5.2 %quarter.1 = bf16[16,64,128]{2,1,0:T(8,128)(2,1)} custom-call(bf16[32,64,512]{2,1,0:T(8,128)(2,1)} %charges.5, bf16[32,64,512]{2,1,0:T(8,128)(2,1)} %projection.1), custom_call_target="tpu_custom_call" | custom-call | tf_op jit(solution)/shard_map/quarter/pallas_call | solution.py:566
  7.7 43.5 %gather.1 = (bf16[16,32,32,128]{3,2,1,0:T(8,128)(2,1)}, bf16[32,32,512]{2,1,0:T(8,128)(2,1)}, bf16[32,64,512]{2,1,0:T(8,128)(2,1)}, s32[32,256]{1,0:T(8,128)}, b...) custom-call(bf16[32,32,512]{2,1,0:T(8,128)(2,1)} %points.3, ...), custom_call_target="tpu_custom_call" | custom-call | tf_op jit(solution)/shard_map/gather/pallas_call | solution.py:574
  51.2 2.5 %table.1 = s32[64,128]{1,0:T(8,128)} custom-call(s32[64,8,128]{2,1,0:T(8,128)} %get-tuple-element.12.ids_all), custom_call_target="tpu_custom_call" | custom-call | tf_op jit(solution)/shard_map/table/pallas_call | solution.py:591
  53.7 84.9 %pairs.1 = f32[512,64,128]{2,1,0:T(8,128)} custom-call(s32[64,128]{1,0:T(8,128)} %table.1, bf16[16,32,32,128]{3,2,1,0:T(8,128)(2,1)} %get-tuple-element.13.x_all, bf16[32,32,512]{2,1,0:T(8,128)(2,1)} %points.3, bf16[32,64,512]{2,1,0:T(8,128)(2,1)} %charges.5, bf16[16,64,128]{2,1,0:T(8,128)(2,1)} %quarter.1, s32[32,256]{1,0:T(8,128)} %index.3, ...), custom_call_target="tpu_custom_call" | custom-call | tf_op jit(solution)/shard_map/pairs/pallas_call | solution.py:599
  138.6 61.8 %reduce.1 = f32[32,64,128]{2,1,0:T(8,128)} custom-call(f32[16,32,64,128]{3,2,1,0:T(8,128)} %bitcast.1), custom_call_target="tpu_custom_call" | custom-call | tf_op jit(solution)/shard_map/reduce/pallas_call | solution.py:625
  200.4 2.3 %copy.12 = f32[32,64,128]{2,1,0:T(8,128)} copy(f32[32,64,128]{2,1,0:T(8,128)} %reduce.1) | data formatting | bytes 2097152
  (1 shorter events, 0.0 us)

commit v2 on v1

--- a/solution.py
+++ b/solution.py
@@ -15,6 +15,7 @@
 RING = 4
 NEAR_SLOTS = 6
 FAR_SLOTS = 10
+DUOS = 6
 LIMIT = 62 * 1024 * 1000
 F32 = jnp.float32
 BF16 = jnp.bfloat16
@@ -34,66 +35,40 @@
     return u * RING + v if first_is_x else v * RING + u
 
 
-def quarter_kernel(charges, projection, out):
-    half = charges.shape[0] // 2
-
-    def body(leaf, carry):
-        parts = []
-        for item in (leaf, leaf + half):
-            parts.append(
-                lax.dot_general(
-                    charges[item], projection[item], (((1,), (1,)), ((), ())), preferred_element_type=F32
-                )
-            )
-        out[leaf] = jnp.concatenate(parts, axis=1).astype(BF16)
-        return carry
-
-    lax.fori_loop(0, half, body, 0, unroll=2)
-
-
 def gather_kernel(
-    points, charges, quarter, index, ids,
-    x_all, points_sib, charges_sib, index_sib, quarter_own, quarter_sib, ids_all,
-    send_x, recv_x, send_s, recv_s, send_i, recv_i, local_sem,
+    points, charges, projection, index, ids,
+    y_out, x_out, w_out, charges_sib, ids_all,
+    p_buf, i_buf, c_buf, j_buf, q_buf, x_raw, y_table, x_aug, w_skel,
+    send_x, recv_x, send_s, recv_s, send_i, recv_i, load_sems, out_sems,
 ):
     x, y, core, z = torus_position()
-    n_z = quarter_own.shape[0]
-    leaf_dev, dim, _ = points.shape
-    cols = x_all.shape[3]
+    n_z = q_buf.shape[1]
+    leaf_dev, dim, leaf = points.shape
+    skel = index.shape[1]
+    cols = x_raw.shape[3]
     half, part = leaf_dev // 2, leaf_dev // 4
+    hold = leaf_dev // 2
+    piece = skel // n_z
     me = (x * RING + y) * n_z + z
     n_ids = ids_all.shape[0]
+    here = x * RING + y
+    own_cols = pl.ds(pl.multiple_of(z * cols, cols), cols)
 
     def device(chip, core_at, z_at):
         return (chip * 2 + core_at, z_at)
 
-    own_ids = pltpu.make_async_copy(ids, ids_all.at[me], local_sem)
-    own_ids.start()
-
-    def send_ids(step, carry):
-        peer = lax.rem(me + step, n_ids)
-        pltpu.make_async_remote_copy(
-            src_ref=ids, dst_ref=ids_all.at[me], send_sem=send_i, recv_sem=recv_i,
-            device_id=device(peer // n_z, core, lax.rem(peer, n_z)), device_id_type=MESH,
-        ).start()
-        return carry
-
-    lax.fori_loop(1, n_ids, send_ids, 0)
-
     sends = []
 
     def message(kind, sems, src, dst, target):
-        copy = pltpu.make_async_remote_copy(
+        return pltpu.make_async_remote_copy(
             src_ref=src, dst_ref=dst, send_sem=sems[0].at[kind], recv_sem=sems[1].at[kind],
             device_id=target, device_id_type=MESH,
         )
-        return copy
 
     def start(copy):
         copy.start()
         sends.append(copy)
 
-    here = x * RING + y
     side = (send_s, recv_s)
     line = (send_x, recv_x)
 
@@ -101,10 +76,9 @@
     for half_at in range(2):
         first_x = half_at == 0
         u, v = (x, y) if first_x else (y, x)
-        base = half_at * half
-        rows = pl.ds(base, half)
-        src = points.at[rows, :, pl.ds(pl.multiple_of(z * cols, cols), cols)]
-        dst = x_all.at[here, rows]
+        rows = pl.ds(half_at * half, half)
+        src = points.at[rows, :, own_cols]
+        dst = x_raw.at[here, rows]
         kinds = 20 * half_at
         own_x.append(
             [
@@ -118,25 +92,65 @@
         for half_at in range(2):
             start(own_x[half_at][at])
 
-    z_copies = []
-    for step in range(1, n_z):
-        copy = message(step, side, quarter, quarter_own.at[z], device(here, core, lax.rem(z + step, n_z)))
-        start(copy)
-        z_copies.append(copy)
+    loads = []
+    for at, (src, dst) in enumerate(
+        (
+            (charges, c_buf),
+            (projection, j_buf),
+            (points, p_buf.at[0]),
+            (index, i_buf.at[0]),
+            (points.at[:, :, own_cols], x_raw.at[here]),
+            (ids, ids_all.at[me]),
+        )
+    ):
+        copy = pltpu.make_async_copy(src, dst, load_sems.at[at])
+        copy.start()
+        loads.append(copy)
+
     sib_copies = []
-    for at, (src, dst) in enumerate(((points, points_sib), (charges, charges_sib), (index, index_sib))):
+    for at, (src, dst) in enumerate(((points, p_buf.at[1]), (index, i_buf.at[1]), (charges, charges_sib))):
         copy = message(8 + at, side, src, dst, device(here, 1 - core, z))
         start(copy)
         sib_copies.append(copy)
-    copy = message(0, side, quarter, quarter_sib.at[z], device(here, 1 - core, z))
+
+    def send_ids(step, carry):
+        peer = lax.rem(me + step, n_ids)
+        pltpu.make_async_remote_copy(
+            src_ref=ids, dst_ref=ids_all.at[me], send_sem=send_i, recv_sem=recv_i,
+            device_id=device(peer // n_z, core, lax.rem(peer, n_z)), device_id_type=MESH,
+        ).start()
+        return carry
+
+    lax.fori_loop(1, n_ids, send_ids, 0)
+
+    loads[0].wait()
+    loads[1].wait()
+
+    def charge(item, carry):
+        parts = []
+        for at in (item, item + hold):
+            parts.append(
+                lax.dot_general(c_buf[at], j_buf[at], (((1,), (1,)), ((), ())), preferred_element_type=F32)
+            )
+        q_buf[0, z, item] = jnp.concatenate(parts, axis=1).astype(BF16)
+        return carry
+
+    lax.fori_loop(0, hold, charge, 0, unroll=2)
+    z_copies = []
+    own_quarter = q_buf.at[0, z]
+    for step in range(1, n_z):
+        copy = message(step, side, own_quarter, own_quarter, device(here, core, lax.rem(z + step, n_z)))
+        start(copy)
+        z_copies.append(copy)
+    copy = message(0, side, own_quarter, q_buf.at[1, z], device(here, 1 - core, z))
     start(copy)
-    sib_copies.append(copy)
+    sib_quarters = [copy]
 
     def item(half_at, du, dv, quarter_at=None):
         first_x = half_at == 0
         u, v = (x, y) if first_x else (y, x)
         rows = pl.ds(half_at * half, half) if quarter_at is None else pl.ds(half_at * half + quarter_at * part, part)
-        return x_all.at[pick(first_x, wrap(u + du), wrap(v + dv)), rows]
+        return x_raw.at[pick(first_x, wrap(u + du), wrap(v + dv)), rows]
 
     def target(half_at, du, dv):
         first_x = half_at == 0
@@ -160,6 +174,64 @@
         arrived(half_at, 5 + 4 * slot, item(half_at, du, 1))
         forward(half_at, 7 + 4 * slot, item(half_at, du, 1, 1), 0, -1)
 
+    pad = jnp.zeros((16, cols), BF16)
+
+    def widen(half_at, du, dv):
+        first_x = half_at == 0
+        u, v = (x, y) if first_x else (y, x)
+        chip = pick(first_x, wrap(u + du), wrap(v + dv))
+        base = half_at * half
+
+        def body(at, carry):
+            coords = x_raw[chip, base + at]
+            x_aug[chip, base + at] = jnp.concatenate([coords, norm_rows(coords, True), pad], axis=0)
+            return carry
+
+        lax.fori_loop(0, half, body, 0, unroll=4)
+
+    wide_pad = jnp.zeros((16, leaf), BF16)
+    point_number = lax.broadcasted_iota(jnp.int32, (leaf, skel), 0)
+    sources = 2 * leaf_dev
+
+    def source(at_side, first, count):
+        def body(at, carry):
+            coords = p_buf[at_side, at]
+            block = jnp.concatenate([coords + coords, norm_rows(coords, False), wide_pad], axis=0)
+            block = jnp.concatenate([block, block], axis=0)
+            turned = block.T
+            row = at_side * leaf_dev + at
+            y_table[row] = turned[:skel]
+            y_table[sources + row] = turned[skel:]
+            chosen = point_number == i_buf[at_side, pl.ds(at, 1), :]
+            chosen = jnp.where(chosen, 1.0, 0.0).astype(BF16)
+            picked = jnp.dot(block, chosen, preferred_element_type=F32).astype(BF16)
+            y_table[2 * sources + row] = picked.T
+            return carry
+
+        lax.fori_loop(first, first + count, body, 0, unroll=2)
+
+    outs = []
+
+    def put(src, dst):
+        copy = pltpu.make_async_copy(src, dst, out_sems.at[len(outs)])
+        copy.start()
+        outs.append(copy)
+
+    def put_y(at_side):
+        for block in range(3):
+            rows = pl.ds(block * sources + at_side * leaf_dev, leaf_dev)
+            put(y_table.at[rows], y_out.at[rows])
+
+    def assemble(at_side):
+        def body(at, carry):
+            chunks = [q_buf[at_side, step, at] for step in range(n_z)]
+            for half_at in range(2):
+                pieces = [chunk[:, half_at * piece : (half_at + 1) * piece] for chunk in chunks]
+                w_skel[at_side * leaf_dev + half_at * hold + at] = jnp.concatenate(pieces, axis=1)
+            return carry
+
+        lax.fori_loop(0, hold, body, 0, unroll=2)
+
     for half_at in range(2):
         arrived(half_at, 0, item(half_at, -1, 0))
         forward(half_at, 2, item(half_at, -1, 0, 0), 1, 0)
@@ -170,29 +242,55 @@
         across(half_at, 2, 1)
     for half_at in range(2):
         relay(half_at, 0, 0)
+    loads[2].wait()
+    loads[3].wait()
+    loads[4].wait()
+    source(0, 0, leaf_dev // 2)
+    for half_at in range(2):
+        arrived(half_at, 2, item(half_at, 2, 0, 0))
+        arrived(half_at, 3, item(half_at, 2, 0, 1))
+        across(half_at, 3, 2)
     for step in range(1, n_z):
         z_copies[step - 1].wait_recv()
         slot = lax.rem(z - step + n_z, n_z)
-        ref = quarter_own.at[slot]
-        copy = message(4 + step, side, ref, quarter_sib.at[slot], device(here, 1 - core, z))
+        copy = message(4 + step, side, q_buf.at[0, slot], q_buf.at[1, slot], device(here, 1 - core, z))
         start(copy)
-        sib_copies.append(copy)
-    for half_at in range(2):
-        arrived(half_at, 2, item(half_at, 2, 0, 0))
-        arrived(half_at, 3, item(half_at, 2, 0, 1))
-        across(half_at, 3, 2)
-    for slot, du in ((1, -1), (2, 1), (3, 2)):
-        for half_at in range(2):
-            relay(half_at, slot, du)
+        sib_quarters.append(copy)
+    source(0, leaf_dev // 2, leaf_dev // 2)
+    put_y(0)
+    for half_at in range(2):
+        relay(half_at, 1, -1)
+    sib_copies[0].wait_recv()
+    sib_copies[1].wait_recv()
+    source(1, 0, leaf_dev // 2)
+    for half_at in range(2):
+        relay(half_at, 2, 1)
+    source(1, leaf_dev // 2, leaf_dev // 2)
+    put_y(1)
+    for half_at in range(2):
+        for du in (0, -1, 1, 2):
+            widen(half_at, du, 0)
+    for half_at in range(2):
+        relay(half_at, 3, 2)
+    assemble(0)
+    for copy in sib_quarters:
+        copy.wait_recv()
+    assemble(1)
+    put(w_skel, w_out)
+    for half_at in range(2):
+        for dv in (-1, 1):
+            for du in (0, -1, 1, 2):
+                widen(half_at, du, dv)
     for slot, du in ((0, 0), (1, -1), (2, 1), (3, 2)):
         for half_at in range(2):
             arrived(half_at, 6 + 4 * slot, item(half_at, du, 2, 0))
             arrived(half_at, 7 + 4 * slot, item(half_at, du, 2, 1))
-    for copy in sib_copies:
-        copy.wait_recv()
+            widen(half_at, du, 2)
+    put(x_aug, x_out)
+    sib_copies[2].wait_recv()
     for copy in sends:
         copy.wait_send()
-    own_ids.wait()
+    loads[5].wait()
     others = ids_all.at[pl.ds(0, n_ids - 1)]
     every = pltpu.make_async_remote_copy(
         src_ref=others, dst_ref=others, send_sem=send_i, recv_sem=recv_i,
@@ -200,6 +298,8 @@
     )
     every.wait_send()
     every.wait_recv()
+    for copy in outs:
+        copy.wait()
 
 
 def table_kernel(leaf_dev, near_dev, far_dev, n_z, ids_all, table):
@@ -216,7 +316,7 @@
         named = lax.div(ids, 2 * leaf_dev)
         member = jnp.logical_and(named == chip, ids >= 0)
         source = lax.rem(lax.rem(ids, 2 * leaf_dev) + core * leaf_dev, 2 * leaf_dev)
-        code = (lax.div(row, n_z) * leaf_dev + lax.div(lane, per_leaf)) * (2 * leaf_dev) + source
+        code = (lax.div(row, n_z) * leaf_dev + lax.div(lane, per_leaf)) * 256 + source + at * 4 * leaf_dev
         flags = jnp.where(member, 1.0, 0.0)
         upto = jnp.dot(flags.astype(BF16), upper, preferred_element_type=F32).astype(jnp.int32)
         for slot in range(slots):
@@ -246,129 +346,71 @@
 
 
 def pair_kernel(
-    table, x_all, points, charges, quarter, index, points_sib, charges_sib, index_sib, quarter_own, quarter_sib,
+    table, y_in, x_in, w_in, charges, charges_sib,
     out,
-    x_raw, x_aug, y_table, w_table, p_buf, i_buf, q_buf, acc, s_a, s_b, items, sems,
+    x_aug, y_table, w_table, acc, s_a, s_b, items, ends, sems, out_sem,
 ):
-    x, y, core, z = torus_position()
-    chips, leaf_dev, dim, cols = x_all.shape
-    leaf = points.shape[2]
-    skel = index.shape[1]
-    n_z = quarter_own.shape[0]
-    here = x * RING + y
+    leaf_dev, rhs, _ = charges.shape
+    skel = y_in.shape[1]
+    targets, _, cols = x_in.shape
+    n_z = table.shape[0] // (targets // leaf_dev)
     sources = 2 * leaf_dev
-    targets = chips * leaf_dev
-    hold = leaf_dev // 2
-    piece = skel // n_z
 
     loads = []
 
-    def load(at, src, dst):
-        copy = pltpu.make_async_copy(src, dst, sems.at[at])
+    def load(src, dst):
+        copy = pltpu.make_async_copy(src, dst, sems.at[len(loads)])
         copy.start()
         loads.append(copy)
 
-    load(0, points, p_buf.at[0])
-    load(1, points_sib, p_buf.at[1])
-    load(2, index, i_buf.at[0])
-    load(3, index_sib, i_buf.at[1])
-    load(4, quarter_own, q_buf.at[0])
-    load(5, quarter_sib, q_buf.at[1])
-    load(6, x_all, x_raw)
-    at = 8
+    load(x_in, x_aug)
+    load(y_in, y_table)
+    load(w_in, w_table.at[pl.ds(2 * sources, sources)])
     for side, ref in ((0, charges), (1, charges_sib)):
         for half in range(2):
             load(
-                at, ref.at[:, :, pl.ds(half * skel, skel)],
+                ref.at[:, :, pl.ds(half * skel, skel)],
                 w_table.at[pl.ds(half * sources + side * leaf_dev, leaf_dev)],
             )
-            at += 1
-
-    rows = table.shape[0]
-    span = 3 * sources
-
-    def fill(row, count):
-        for slot in range(NEAR_SLOTS):
-            code = table[row, slot]
-            base = lax.div(code, sources) * 256 + lax.rem(code, sources)
-            items[count + 2 * slot] = base
-            items[count + 2 * slot + 1] = base + sources
-        count = count + 2 * table[row, NEAR_SLOTS + FAR_SLOTS]
-        for slot in range(FAR_SLOTS):
-            code = table[row, NEAR_SLOTS + slot]
-            items[count + slot] = lax.div(code, sources) * 256 + lax.rem(code, sources) + 2 * sources
-        return count + table[row, NEAR_SLOTS + FAR_SLOTS + 1]
-
-    count = lax.fori_loop(0, rows, fill, 0)
-    for at in range(12):
+
+    def fill(chip, count):
+        for step in range(n_z):
+            row = chip * n_z + step
+            for slot in range(NEAR_SLOTS):
+                code = table[row, slot]
+                items[count + 2 * slot] = code
+                items[count + 2 * slot + 1] = code + sources
+            count = count + 2 * table[row, NEAR_SLOTS + FAR_SLOTS]
+            for slot in range(FAR_SLOTS):
+                items[count + slot] = table[row, NEAR_SLOTS + slot]
+            count = count + table[row, NEAR_SLOTS + FAR_SLOTS + 1]
+        ends[chip] = count
+        return count
+
+    chips = table.shape[0] // n_z
+    count = lax.fori_loop(0, chips, fill, 0)
+    for at in range(6 * DUOS):
         items[count + at] = targets * 256
-
-    for copy in loads:
-        copy.wait()
-    copy = pltpu.make_async_copy(quarter, q_buf.at[0, z], sems.at[7])
-    copy.start()
-    own = pltpu.make_async_copy(
-        points.at[:, :, pl.ds(pl.multiple_of(z * cols, cols), cols)], x_raw.at[here], sems.at[6]
-    )
-    own.start()
 
     def zero(at, carry):
         acc[at] = jnp.zeros(acc.shape[1:], F32)
         return carry
 
     lax.fori_loop(0, targets + 1, zero, 0, unroll=4)
-    copy.wait()
-    own.wait()
-
-    pad = jnp.zeros((16, cols), BF16)
-
-    def widen(at, carry):
-        coords = x_raw[lax.div(at, leaf_dev), lax.rem(at, leaf_dev)]
-        x_aug[at] = jnp.concatenate([coords, norm_rows(coords, True), pad], axis=0)
-        return carry
-
-    lax.fori_loop(0, targets, widen, 0, unroll=4)
-
-    wide_pad = jnp.zeros((16, leaf), BF16)
-    point_number = lax.broadcasted_iota(jnp.int32, (leaf, skel), 0)
-
-    def source(at, carry):
-        side, item = lax.div(at, leaf_dev), lax.rem(at, leaf_dev)
-        coords = p_buf[side, item]
-        block = jnp.concatenate([coords + coords, norm_rows(coords, False), wide_pad], axis=0)
-        block = jnp.concatenate([block, block], axis=0)
-        turned = block.T
-        y_table[at] = turned[:skel]
-        y_table[sources + at] = turned[skel:]
-        chosen = point_number == i_buf[side, pl.ds(item, 1), :]
-        chosen = jnp.where(chosen, 1.0, 0.0).astype(BF16)
-        picked = jnp.dot(block, chosen, preferred_element_type=F32).astype(BF16)
-        y_table[2 * sources + at] = picked.T
-        return carry
-
-    lax.fori_loop(0, sources, source, 0, unroll=2)
-
-    def assemble(at, carry):
-        side, item = lax.div(at, hold), lax.rem(at, hold)
-        chunks = [q_buf[side, step, item] for step in range(n_z)]
-        for half in range(2):
-            pieces = [chunk[:, half * piece : (half + 1) * piece] for chunk in chunks]
-            w_table[2 * sources + side * leaf_dev + half * hold + item] = jnp.concatenate(pieces, axis=1)
-        return carry
-
-    lax.fori_loop(0, 2 * hold, assemble, 0, unroll=2)
+    for copy in loads:
+        copy.wait()
 
     empty = jnp.zeros((64, cols), BF16)
     low_lanes = lax.broadcasted_iota(jnp.int32, (skel, 128), 1) < 64
 
     def read(at):
         code = items[at]
-        return lax.div(code, 256), lax.rem(code, 256)
-
-    def scores(group, buf):
-        for duo in range(2):
-            t_0, u_0 = read(group * 4 + 2 * duo)
-            t_1, u_1 = read(group * 4 + 2 * duo + 1)
+        return lax.shift_right_logical(code, 8), jnp.bitwise_and(code, 255)
+
+    def scores(group, buf, at):
+        for duo in [at]:
+            t_0, u_0 = read(group * 2 * DUOS + 2 * duo)
+            t_1, u_1 = read(group * 2 * DUOS + 2 * duo + 1)
             x_0 = x_aug[jnp.minimum(t_0, targets - 1)]
             x_1 = x_aug[jnp.minimum(t_1, targets - 1)]
             right = jnp.concatenate(
@@ -377,10 +419,10 @@
             left = jnp.where(low_lanes, y_table[u_0], y_table[u_1])
             buf[duo] = jnp.dot(left, right, preferred_element_type=F32)
 
-    def sums(group, buf):
-        for duo in range(2):
-            t_0, u_0 = read(group * 4 + 2 * duo)
-            t_1, u_1 = read(group * 4 + 2 * duo + 1)
+    def sums(group, buf, at):
+        for duo in [at]:
+            t_0, u_0 = read(group * 2 * DUOS + 2 * duo)
+            t_1, u_1 = read(group * 2 * DUOS + 2 * duo + 1)
             kernel = jnp.exp(buf[duo]).astype(BF16)
             weights = jnp.concatenate([w_table[u_0], w_table[u_1]], axis=0)
             terms = jnp.dot(weights, kernel, preferred_element_type=F32)
@@ -388,19 +430,35 @@
             acc[t_0] = acc[t_0] + terms[:rhs, :cols]
             acc[t_1] = acc[t_1] + terms[rhs:, cols:]
 
-    scores(0, s_a)
-
-    def step(at, carry):
-        scores(2 * at + 1, s_b)
-        sums(2 * at, s_a)
-        scores(2 * at + 2, s_a)
-        sums(2 * at + 1, s_b)
+    for duo in range(DUOS):
+        scores(0, s_a, duo)
+
+    def store(chip):
+        rows = pl.ds(pl.multiple_of(chip * leaf_dev, leaf_dev), leaf_dev)
+        return pltpu.make_async_copy(acc.at[rows], out.at[rows], out_sem)
+
+    def step(at, chip):
+        for duo in range(DUOS):
+            sums(2 * at, s_a, duo)
+            scores(2 * at + 1, s_b, duo)
+        for duo in range(DUOS):
+            sums(2 * at + 1, s_b, duo)
+            scores(2 * at + 2, s_a, duo)
+        full = jnp.logical_and(chip < chips, ends[jnp.minimum(chip, chips - 1)] <= (at + 1) * 4 * DUOS)
+
+        @pl.when(full)
+        def _():
+            store(chip).start()
+
+        return jnp.where(full, chip + 1, chip)
+
+    def flush(chip, carry):
+        store(chip).start()
         return carry
 
-    lax.fori_loop(0, lax.div(count + 7, 8), step, 0)
-    done = pltpu.make_async_copy(acc.at[pl.ds(0, targets)], out, sems.at[0])
-    done.start()
-    done.wait()
+    chip = lax.fori_loop(0, lax.div(count + 4 * DUOS - 1, 4 * DUOS), step, 0)
+    lax.fori_loop(chip, chips, flush, 0)
+    pltpu.make_async_copy(acc.at[pl.ds(0, targets)], out, out_sem).wait()
 
 
 def reduce_kernel(
@@ -480,7 +538,7 @@
             kind = half_at * 10 + 2 * at
             send(part, kind, chip_at(half_at, 1, 0), lambda row: held[slot, base + row])
             send(part, kind + 1, chip_at(half_at, -1, 0), lambda row: held[slot, base + part + row])
-    for dv, at in order:
+    def pass_on(dv, at):
         for half_at in range(2):
             base = half_at * half
             for du, side in ((1, 0), (-1, 1)):
@@ -496,7 +554,8 @@
 
                 lax.fori_loop(0, part, add, 0, unroll=2)
                 send(half, kind, chip_at(half_at, du, 0), lambda row: held[slot, base + row])
-    for dv, at in order:
+
+    def second_axis(dv, at):
         for half_at in range(2):
             base = half_at * half
             ready(half_at, 0, dv)
@@ -528,6 +587,12 @@
 
                 lax.fori_loop(0, part, add_late, 0, unroll=2)
                 send(half, late, chip_at(half_at, 0, dv), lambda row: held[slot, base + row])
+
+    for step, (dv, at) in enumerate(order):
+        pass_on(dv, at)
+        if step > 0:
+            second_axis(*order[step - 1])
+    second_axis(*order[-1])
     for half_at in range(2):
         base = half_at * half
         slot = chip_at(half_at, 0, 0)
@@ -563,31 +628,33 @@
 
     ids = jnp.concatenate([row_of(near_ids), row_of(far_ids), jnp.full((6, 128), -1, jnp.int32)], axis=0)
 
-    quarter = pl.pallas_call(
-        quarter_kernel,
-        out_shape=shape((leaf_dev // 2, rhs, 2 * skel // n_z), BF16),
-        in_specs=[VMEM, VMEM],
-        out_specs=VMEM,
-        name="quarter",
-        compiler_params=params(),
-    )(charges, projection)
-    x_all, points_sib, charges_sib, index_sib, quarter_own, quarter_sib, ids_all = pl.pallas_call(
+    quarter = (leaf_dev // 2, rhs, 2 * skel // n_z)
+    y_table, x_aug, w_skel, charges_sib, ids_all = pl.pallas_call(
         gather_kernel,
         out_shape=[
-            shape((chips, leaf_dev, dim, cols), BF16),
-            shape(points.shape, BF16),
+            shape((3 * sources, skel, 128), BF16),
+            shape((chips, leaf_dev, 64, cols), BF16),
+            shape((sources, rhs, skel), BF16),
             shape(charges.shape, BF16),
-            shape(skeleton_index.shape, jnp.int32),
-            shape((n_z,) + quarter.shape, BF16),
-            shape((n_z,) + quarter.shape, BF16),
             shape((chips * n_z, 8, 128), jnp.int32),
         ],
         in_specs=[ANY] * 5,
-        out_specs=[ANY] * 7,
-        scratch_shapes=[dma((40,)), dma((40,)), dma((12,)), dma((12,)), dma, dma, dma],
+        out_specs=[ANY] * 5,
+        scratch_shapes=[
+            pltpu.VMEM((2,) + points.shape, BF16),
+            pltpu.VMEM((2,) + skeleton_index.shape, jnp.int32),
+            pltpu.VMEM(charges.shape, BF16),
+            pltpu.VMEM(projection.shape, BF16),
+            pltpu.VMEM((2, n_z) + quarter, BF16),
+            pltpu.VMEM((chips, leaf_dev, dim, cols), BF16),
+            pltpu.VMEM((3 * sources, skel, 128), BF16),
+            pltpu.VMEM((chips, leaf_dev, 64, cols), BF16),
+            pltpu.VMEM((sources, rhs, skel), BF16),
+            dma((40,)), dma((40,)), dma((12,)), dma((12,)), dma, dma, dma((6,)), dma((8,)),
+        ],
         name="gather",
         compiler_params=params(has_side_effects=True),
-    )(points, charges, quarter, skeleton_index, ids)
+    )(points, charges, projection, skeleton_index, ids)
     table = pl.pallas_call(
         functools.partial(table_kernel, leaf_dev, near_dev, far_dev, n_z),
         out_shape=shape((chips * n_z, 128), jnp.int32),
@@ -599,28 +666,23 @@
     partial_sums = pl.pallas_call(
         pair_kernel,
         out_shape=shape((targets, rhs, cols), F32),
-        in_specs=[SMEM] + [ANY] * 10,
+        in_specs=[SMEM] + [ANY] * 5,
         out_specs=ANY,
         scratch_shapes=[
-            pltpu.VMEM((chips, leaf_dev, dim, cols), BF16),
             pltpu.VMEM((targets, 64, cols), BF16),
             pltpu.VMEM((3 * sources, skel, 128), BF16),
             pltpu.VMEM((3 * sources, rhs, skel), BF16),
-            pltpu.VMEM((2,) + points.shape, BF16),
-            pltpu.VMEM((2,) + skeleton_index.shape, jnp.int32),
-            pltpu.VMEM((2, n_z) + quarter.shape, BF16),
             pltpu.VMEM((targets + 1, rhs, cols), F32),
-            pltpu.VMEM((2, skel, 2 * cols), F32),
-            pltpu.VMEM((2, skel, 2 * cols), F32),
-            pltpu.SMEM((chips * n_z * (2 * NEAR_SLOTS + FAR_SLOTS) + 32,), jnp.int32),
-            dma((16,)),
+            pltpu.VMEM((DUOS, skel, 2 * cols), F32),
+            pltpu.VMEM((DUOS, skel, 2 * cols), F32),
+            pltpu.SMEM((chips * n_z * (2 * NEAR_SLOTS + FAR_SLOTS) + 8 * DUOS,), jnp.int32),
+            pltpu.SMEM((chips,), jnp.int32),
+            dma((8,)),
+            dma,
         ],
         name="pairs",
         compiler_params=params(),
-    )(
-        table, x_all, points, charges, quarter, skeleton_index, points_sib, charges_sib, index_sib, quarter_own,
-        quarter_sib,
-    )
+    )(table, y_table, x_aug.reshape(targets, 64, cols), w_skel, charges, charges_sib)
     half, part = leaf_dev // 2, leaf_dev // 4
     return pl.pallas_call(
         reduce_kernel,

time: 203 us -> 165 us (0.81)
  Pallas kernels: 198 us -> 159 us
    pallas_call x1, Pallas kernels: 84.9 us -> 45.8 us  [per_device(): pl.pallas_call(pair_kernel, out_shape=shape((targets, rhs, cols), F32), i...]
    pallas_call x2 -> x1, Pallas kernels: 48.7 us -> 51.9 us  [per_device(): pl.pallas_call(gather_kernel, out_shape=[shape((3 * sources, skel, 128),...]
    pallas_call x1, Pallas kernels: 61.8 us -> 59.1 us  [per_device(): pl.pallas_call(reduce_kernel, out_shape=shape((leaf_dev, rhs, cols), F32)...]
where the time goes in v2:
time: 165 us; the launch traced here: 164 us
  Pallas kernels  159 us (96%)
  local copies, waits for them, and re-layouts  4.12 us (2%)
    pallas_call x1, Pallas kernels, per_device(): pl.pallas_call(reduce_kernel, out_shape=shape((leaf_dev, rhs, cols), F32)...  59.1 us
    pallas_call x1, Pallas kernels, per_device(): pl.pallas_call(gather_kernel, out_shape=[shape((3 * sources, skel, 128),...  51.9 us
    pallas_call x1, Pallas kernels, per_device(): pl.pallas_call(pair_kernel, out_shape=shape((targets, rhs, cols), F32), i...  45.8 us
    unnamed x3, local copies, waits for them, and re-layouts  3.83 us

profile of v2, /device:TPU:0, one launch (start us, length us, event | category | flops | bytes accessed | tf_op | source)
XLA Modules:
  0.0 164.1 jit_solution(15869134042921729650)
XLA Ops:
  0.0 0.1 pad.7.clone
  0.1 0.8 copy.9
  0.8 0.1 reshape.12
  0.9 0.8 copy.10
  1.7 0.1 reshape.13
  1.8 0.7 fusion.ids
  2.5 51.9 %gather.1 = (bf16[192,256,128]{2,1,0:T(8,128)(2,1)}, bf16[16,32,64,128]{3,2,1,0:T(8,128)(2,1)}, bf16[64,64,256]{2,1,0:T(8,128)(2,1)}, bf16[32,64,512]{2,1,0:T(8,128)(2,1)}, s32[64,8,128]{2,1,0:T(8,128)}) custom-call(bf16[32,32,512]{2,1,0:T(8,128)(2,1)} %points.1, bf16[32,64,512]{2,1,0:T(8,128)(2,1)} %charges.3, bf16[32,64,512]{2,1,0:T(8,128)(2,1)} %projection.1, ...), custom_call_target="tpu_custom_call" | custom-call | tf_op jit(solution)/shard_map/gather/pallas_call | solution.py:632
  54.4 2.5 %table.1 = s32[64,128]{1,0:T(8,128)} custom-call(s32[64,8,128]{2,1,0:T(8,128)} %get-tuple-element.10.ids_all), custom_call_target="tpu_custom_call" | custom-call | tf_op jit(solution)/shard_map/table/pallas_call | solution.py:658
  56.9 45.8 %pairs.1 = f32[512,64,128]{2,1,0:T(8,128)} custom-call(s32[64,128]{1,0:T(8,128)} %table.1, bf16[192,256,128]{2,1,0:T(8,128)(2,1)} %get-tuple-element.11.y_in, bf16[512,64,128]{2,1,0:T(8,128)(2,1)} %bitcast.3, bf16[64,64,256]{2,1,0:T(8,128)(2,1)} %get-tuple-element.13.w_in, bf16[32,64,512]{2,1,0:T(8,128)(2,1)} %charges.3, ...), custom_call_target="tpu_custom_call" | custom-call | tf_op jit(solution)/shard_map/pairs/pallas_call | solution.py:666
  102.7 59.1 %reduce.1 = f32[32,64,128]{2,1,0:T(8,128)} custom-call(f32[16,32,64,128]{3,2,1,0:T(8,128)} %bitcast.2), custom_call_target="tpu_custom_call" | custom-call | tf_op jit(solution)/shard_map/reduce/pallas_call | solution.py:687
  161.8 2.3 %copy.12 = f32[32,64,128]{2,1,0:T(8,128)} copy(f32[32,64,128]{2,1,0:T(8,128)} %reduce.1) | data formatting | bytes 2097152
  (1 shorter events, 0.0 us)

commit v3 on v2

--- a/solution.py
+++ b/solution.py
@@ -10,8 +10,8 @@
 
 MESH = pl.DeviceIdType.MESH
 ANY = pl.BlockSpec(memory_space=pl.ANY)
+HBM = pl.BlockSpec(memory_space=pltpu.HBM)
 VMEM = pl.BlockSpec(memory_space=pltpu.VMEM)
-SMEM = pl.BlockSpec(memory_space=pltpu.SMEM)
 RING = 4
 NEAR_SLOTS = 6
 FAR_SLOTS = 10
@@ -35,11 +35,56 @@
     return u * RING + v if first_is_x else v * RING + u
 
 
+def chip_table(leaf_dev, near_dev, far_dev, n_z, chip, core, ids_all):
+    rows = ids_all.shape[0]
+    lane = lax.broadcasted_iota(jnp.int32, (rows, 128), 1)
+    row = lax.broadcasted_iota(jnp.int32, (rows, 128), 0)
+    upper = lax.broadcasted_iota(jnp.int32, (128, 128), 0) <= lax.broadcasted_iota(jnp.int32, (128, 128), 1)
+    upper = jnp.where(upper, 1.0, 0.0).astype(BF16)
+    result = jnp.zeros((rows, 128), jnp.int32)
+    for at, (per_leaf, slots, start) in enumerate(((near_dev, NEAR_SLOTS, 0), (far_dev, FAR_SLOTS, NEAR_SLOTS))):
+        first = 0 if at == 0 else near_dev
+        pieces = [ids_all[:, first + step, :leaf_dev] for step in range(per_leaf)]
+        if per_leaf * leaf_dev < 128:
+            pieces.append(jnp.full((rows, 128 - per_leaf * leaf_dev), -1, jnp.int32))
+        ids = jnp.concatenate(pieces, axis=1)
+        named = lax.div(ids, 2 * leaf_dev)
+        member = jnp.logical_and(named == chip, ids >= 0)
+        source = lax.rem(lax.rem(ids, 2 * leaf_dev) + core * leaf_dev, 2 * leaf_dev)
+        code = (lax.div(row, n_z) * leaf_dev + lax.rem(lane, leaf_dev)) * 256 + source + at * 4 * leaf_dev
+        flags = jnp.where(member, 1.0, 0.0)
+        upto = jnp.dot(flags.astype(BF16), upper, preferred_element_type=F32).astype(jnp.int32)
+        for slot in range(slots):
+            chosen = jnp.logical_and(member, upto == slot + 1)
+            value = jnp.sum(jnp.where(chosen, code, 0), axis=1, keepdims=True)
+            result = jnp.where(lane == start + slot, value, result)
+        count = jnp.sum(jnp.where(member, 1, 0), axis=1, keepdims=True)
+        result = jnp.where(lane == NEAR_SLOTS + FAR_SLOTS + at, count, result)
+    return result
+
+
+def norm_rows(coords, sign_first):
+    values = coords.astype(F32)
+    norm = -jnp.sum(values * values, axis=0, keepdims=True)
+    high = norm.astype(BF16).astype(F32)
+    rest = norm - high
+    middle = rest.astype(BF16).astype(F32)
+    low = rest - middle
+    shape = (16, coords.shape[1])
+    row = lax.broadcasted_iota(jnp.int32, shape, 0)
+    start = 0 if sign_first else 3
+    ones = 3 if sign_first else 0
+    result = jnp.where(jnp.logical_and(row >= ones, row < ones + 3), 1.0, 0.0)
+    for at, piece in enumerate((high, middle, low)):
+        result = jnp.where(row == start + at, jnp.broadcast_to(piece, shape), result)
+    return result.astype(BF16)
+
+
 def gather_kernel(
-    points, charges, projection, index, ids,
-    y_out, x_out, w_out, charges_sib, ids_all,
-    p_buf, i_buf, c_buf, j_buf, q_buf, x_raw, y_table, x_aug, w_skel,
-    send_x, recv_x, send_s, recv_s, send_i, recv_i, load_sems, out_sems,
+    near_dev, far_dev, points, charges, projection, index, ids,
+    y_table, x_aug, w_table, table,
+    ids_all, p_buf, i_buf, c_buf, j_buf, q_buf, x_raw,
+    send_x, recv_x, send_s, recv_s, send_i, recv_i, load_sems,
 ):
     x, y, core, z = torus_position()
     n_z = q_buf.shape[1]
@@ -56,6 +101,36 @@
 
     def device(chip, core_at, z_at):
         return (chip * 2 + core_at, z_at)
+
+    barrier = pltpu.get_barrier_semaphore()
+
+    def greet(step, carry):
+        peer = lax.rem(me + step, n_ids)
+        pl.semaphore_signal(
+            barrier, inc=1, device_id=device(peer // n_z, core, lax.rem(peer, n_z)), device_id_type=MESH
+        )
+        return carry
+
+    lax.fori_loop(1, n_ids, greet, 0)
+    pl.semaphore_signal(barrier, inc=1, device_id=device(here, 1 - core, z), device_id_type=MESH)
+
+    loads = []
+    for at, (src, dst) in enumerate(
+        (
+            (charges, c_buf),
+            (projection, j_buf),
+            (points, p_buf.at[0]),
+            (index, i_buf.at[0]),
+            (points.at[:, :, own_cols], x_raw.at[here]),
+            (ids, ids_all.at[me]),
+            (charges.at[:, :, pl.ds(0, skel)], w_table.at[pl.ds(0, leaf_dev)]),
+            (charges.at[:, :, pl.ds(skel, skel)], w_table.at[pl.ds(2 * leaf_dev, leaf_dev)]),
+        )
+    ):
+        copy = pltpu.make_async_copy(src, dst, load_sems.at[at])
+        copy.start()
+        loads.append(copy)
+    pl.semaphore_wait(barrier, n_ids)
 
     sends = []
 
@@ -92,23 +167,15 @@
         for half_at in range(2):
             start(own_x[half_at][at])
 
-    loads = []
+    sib_copies = []
     for at, (src, dst) in enumerate(
         (
-            (charges, c_buf),
-            (projection, j_buf),
-            (points, p_buf.at[0]),
-            (index, i_buf.at[0]),
-            (points.at[:, :, own_cols], x_raw.at[here]),
-            (ids, ids_all.at[me]),
+            (points, p_buf.at[1]),
+            (index, i_buf.at[1]),
+            (charges.at[:, :, pl.ds(0, skel)], w_table.at[pl.ds(leaf_dev, leaf_dev)]),
+            (charges.at[:, :, pl.ds(skel, skel)], w_table.at[pl.ds(3 * leaf_dev, leaf_dev)]),
         )
     ):
-        copy = pltpu.make_async_copy(src, dst, load_sems.at[at])
-        copy.start()
-        loads.append(copy)
-
-    sib_copies = []
-    for at, (src, dst) in enumerate(((points, p_buf.at[1]), (index, i_buf.at[1]), (charges, charges_sib))):
         copy = message(8 + at, side, src, dst, device(here, 1 - core, z))
         start(copy)
         sib_copies.append(copy)
@@ -210,24 +277,12 @@
 
         lax.fori_loop(first, first + count, body, 0, unroll=2)
 
-    outs = []
-
-    def put(src, dst):
-        copy = pltpu.make_async_copy(src, dst, out_sems.at[len(outs)])
-        copy.start()
-        outs.append(copy)
-
-    def put_y(at_side):
-        for block in range(3):
-            rows = pl.ds(block * sources + at_side * leaf_dev, leaf_dev)
-            put(y_table.at[rows], y_out.at[rows])
-
     def assemble(at_side):
         def body(at, carry):
             chunks = [q_buf[at_side, step, at] for step in range(n_z)]
             for half_at in range(2):
                 pieces = [chunk[:, half_at * piece : (half_at + 1) * piece] for chunk in chunks]
-                w_skel[at_side * leaf_dev + half_at * hold + at] = jnp.concatenate(pieces, axis=1)
+                w_table[2 * sources + at_side * leaf_dev + half_at * hold + at] = jnp.concatenate(pieces, axis=1)
             return carry
 
         lax.fori_loop(0, hold, body, 0, unroll=2)
@@ -257,7 +312,6 @@
         start(copy)
         sib_quarters.append(copy)
     source(0, leaf_dev // 2, leaf_dev // 2)
-    put_y(0)
     for half_at in range(2):
         relay(half_at, 1, -1)
     sib_copies[0].wait_recv()
@@ -266,7 +320,18 @@
     for half_at in range(2):
         relay(half_at, 2, 1)
     source(1, leaf_dev // 2, leaf_dev // 2)
-    put_y(1)
+    for copy in loads[5:]:
+        copy.wait()
+    sib_copies[2].wait_recv()
+    sib_copies[3].wait_recv()
+    others = ids_all.at[pl.ds(0, n_ids - 1)]
+    every = pltpu.make_async_remote_copy(
+        src_ref=others, dst_ref=others, send_sem=send_i, recv_sem=recv_i,
+        device_id=target(0, 1, 0), device_id_type=MESH,
+    )
+    every.wait_send()
+    every.wait_recv()
+    table[...] = chip_table(leaf_dev, near_dev, far_dev, n_z, here, core, ids_all)
     for half_at in range(2):
         for du in (0, -1, 1, 2):
             widen(half_at, du, 0)
@@ -276,7 +341,6 @@
     for copy in sib_quarters:
         copy.wait_recv()
     assemble(1)
-    put(w_skel, w_out)
     for half_at in range(2):
         for dv in (-1, 1):
             for du in (0, -1, 1, 2):
@@ -286,92 +350,25 @@
             arrived(half_at, 6 + 4 * slot, item(half_at, du, 2, 0))
             arrived(half_at, 7 + 4 * slot, item(half_at, du, 2, 1))
             widen(half_at, du, 2)
-    put(x_aug, x_out)
-    sib_copies[2].wait_recv()
     for copy in sends:
         copy.wait_send()
-    loads[5].wait()
-    others = ids_all.at[pl.ds(0, n_ids - 1)]
-    every = pltpu.make_async_remote_copy(
-        src_ref=others, dst_ref=others, send_sem=send_i, recv_sem=recv_i,
-        device_id=target(0, 1, 0), device_id_type=MESH,
-    )
-    every.wait_send()
-    every.wait_recv()
-    for copy in outs:
-        copy.wait()
-
-
-def table_kernel(leaf_dev, near_dev, far_dev, n_z, ids_all, table):
-    x, y, core, _ = torus_position()
-    chip = x * RING + y
-    rows = ids_all.shape[0]
-    lane = lax.broadcasted_iota(jnp.int32, (rows, 128), 1)
-    row = lax.broadcasted_iota(jnp.int32, (rows, 128), 0)
-    upper = lax.broadcasted_iota(jnp.int32, (128, 128), 0) <= lax.broadcasted_iota(jnp.int32, (128, 128), 1)
-    upper = jnp.where(upper, 1.0, 0.0).astype(BF16)
-    result = jnp.zeros((rows, 128), jnp.int32)
-    for at, (per_leaf, slots, start) in enumerate(((near_dev, NEAR_SLOTS, 0), (far_dev, FAR_SLOTS, NEAR_SLOTS))):
-        ids = ids_all[:, at, :]
-        named = lax.div(ids, 2 * leaf_dev)
-        member = jnp.logical_and(named == chip, ids >= 0)
-        source = lax.rem(lax.rem(ids, 2 * leaf_dev) + core * leaf_dev, 2 * leaf_dev)
-        code = (lax.div(row, n_z) * leaf_dev + lax.div(lane, per_leaf)) * 256 + source + at * 4 * leaf_dev
-        flags = jnp.where(member, 1.0, 0.0)
-        upto = jnp.dot(flags.astype(BF16), upper, preferred_element_type=F32).astype(jnp.int32)
-        for slot in range(slots):
-            chosen = jnp.logical_and(member, upto == slot + 1)
-            value = jnp.sum(jnp.where(chosen, code, 0), axis=1, keepdims=True)
-            result = jnp.where(lane == start + slot, value, result)
-        count = jnp.sum(jnp.where(member, 1, 0), axis=1, keepdims=True)
-        result = jnp.where(lane == NEAR_SLOTS + FAR_SLOTS + at, count, result)
-    table[...] = result
-
-
-def norm_rows(coords, sign_first):
-    values = coords.astype(F32)
-    norm = -jnp.sum(values * values, axis=0, keepdims=True)
-    high = norm.astype(BF16).astype(F32)
-    rest = norm - high
-    middle = rest.astype(BF16).astype(F32)
-    low = rest - middle
-    shape = (16, coords.shape[1])
-    row = lax.broadcasted_iota(jnp.int32, shape, 0)
-    start = 0 if sign_first else 3
-    ones = 3 if sign_first else 0
-    result = jnp.where(jnp.logical_and(row >= ones, row < ones + 3), 1.0, 0.0)
-    for at, piece in enumerate((high, middle, low)):
-        result = jnp.where(row == start + at, jnp.broadcast_to(piece, shape), result)
-    return result.astype(BF16)
-
-
-def pair_kernel(
-    table, y_in, x_in, w_in, charges, charges_sib,
-    out,
-    x_aug, y_table, w_table, acc, s_a, s_b, items, ends, sems, out_sem,
-):
-    leaf_dev, rhs, _ = charges.shape
-    skel = y_in.shape[1]
-    targets, _, cols = x_in.shape
+
+
+def pair_kernel(table_in, y_table, x_aug, w_table, out, acc, s_a, s_b, table, items, ends, out_sem):
+    copy = pltpu.make_async_copy(table_in, table, out_sem)
+    copy.start()
+    skel = y_table.shape[1]
+    targets, _, cols = x_aug.shape
+    leaf_dev = w_table.shape[0] // 6
     n_z = table.shape[0] // (targets // leaf_dev)
     sources = 2 * leaf_dev
 
-    loads = []
-
-    def load(src, dst):
-        copy = pltpu.make_async_copy(src, dst, sems.at[len(loads)])
-        copy.start()
-        loads.append(copy)
-
-    load(x_in, x_aug)
-    load(y_in, y_table)
-    load(w_in, w_table.at[pl.ds(2 * sources, sources)])
-    for side, ref in ((0, charges), (1, charges_sib)):
-        for half in range(2):
-            load(
-                ref.at[:, :, pl.ds(half * skel, skel)],
-                w_table.at[pl.ds(half * sources + side * leaf_dev, leaf_dev)],
-            )
+    def zero(at, carry):
+        acc[at] = jnp.zeros(acc.shape[1:], F32)
+        return carry
+
+    lax.fori_loop(0, targets + 1, zero, 0, unroll=4)
+    copy.wait()
 
     def fill(chip, count):
         for step in range(n_z):
@@ -392,13 +389,6 @@
     for at in range(6 * DUOS):
         items[count + at] = targets * 256
 
-    def zero(at, carry):
-        acc[at] = jnp.zeros(acc.shape[1:], F32)
-        return carry
-
-    lax.fori_loop(0, targets + 1, zero, 0, unroll=4)
-    for copy in loads:
-        copy.wait()
 
     empty = jnp.zeros((64, cols), BF16)
     low_lanes = lax.broadcasted_iota(jnp.int32, (skel, 128), 1) < 64
@@ -475,6 +465,12 @@
         u, v = (x, y) if first_x else (y, x)
         return pick(first_x, wrap(u + du), wrap(v + dv))
 
+    barrier = pltpu.get_barrier_semaphore()
+    for du, dv in ((1, 0), (-1, 0), (0, 1), (0, -1)):
+        pl.semaphore_signal(
+            barrier, inc=1, device_id=(chip_at(0, du, dv) * 2 + core, z), device_id_type=MESH
+        )
+
     loads = {}
     for du, _ in order:
         for dv, _ in order:
@@ -487,6 +483,7 @@
                 copy.start()
                 loads[half_at, du, dv] = copy
 
+    pl.semaphore_wait(barrier, 4)
     sends = []
 
     def wires(size, kind, chip):
@@ -618,71 +615,55 @@
     cols = leaf // n_z
     near_dev, far_dev = near_ids.shape[1], far_ids.shape[1]
     sources, targets = 2 * leaf_dev, chips * leaf_dev
-    params = functools.partial(pltpu.CompilerParams, vmem_limit_bytes=LIMIT)
+    params = pltpu.CompilerParams
     dma = pltpu.SemaphoreType.DMA
     shape = jax.ShapeDtypeStruct
 
-    def row_of(ids):
-        flat = ids.reshape(1, -1)
-        return jnp.pad(flat, ((0, 0), (0, 128 - flat.shape[1])), constant_values=-1)
-
-    ids = jnp.concatenate([row_of(near_ids), row_of(far_ids), jnp.full((6, 128), -1, jnp.int32)], axis=0)
+    ids = jnp.concatenate([near_ids.T, far_ids.T], axis=0)
+    ids = jnp.pad(ids, ((0, 8 - near_dev - far_dev), (0, 128 - leaf_dev)), constant_values=-1)
 
     quarter = (leaf_dev // 2, rhs, 2 * skel // n_z)
-    y_table, x_aug, w_skel, charges_sib, ids_all = pl.pallas_call(
-        gather_kernel,
+    y_table, x_aug, w_table, table = pl.pallas_call(
+        functools.partial(gather_kernel, near_dev, far_dev),
         out_shape=[
-            shape((3 * sources, skel, 128), BF16),
-            shape((chips, leaf_dev, 64, cols), BF16),
-            shape((sources, rhs, skel), BF16),
-            shape(charges.shape, BF16),
-            shape((chips * n_z, 8, 128), jnp.int32),
+            pltpu.VMEM((3 * sources, skel, 128), BF16),
+            pltpu.VMEM((chips, leaf_dev, 64, cols), BF16),
+            pltpu.VMEM((3 * sources, rhs, skel), BF16),
+            pltpu.VMEM((chips * n_z, 128), jnp.int32),
         ],
-        in_specs=[ANY] * 5,
-        out_specs=[ANY] * 5,
+        in_specs=[HBM] * 5,
+        out_specs=[VMEM] * 4,
         scratch_shapes=[
+            pltpu.VMEM((chips * n_z, 8, 128), jnp.int32),
             pltpu.VMEM((2,) + points.shape, BF16),
             pltpu.VMEM((2,) + skeleton_index.shape, jnp.int32),
             pltpu.VMEM(charges.shape, BF16),
             pltpu.VMEM(projection.shape, BF16),
             pltpu.VMEM((2, n_z) + quarter, BF16),
             pltpu.VMEM((chips, leaf_dev, dim, cols), BF16),
-            pltpu.VMEM((3 * sources, skel, 128), BF16),
-            pltpu.VMEM((chips, leaf_dev, 64, cols), BF16),
-            pltpu.VMEM((sources, rhs, skel), BF16),
-            dma((40,)), dma((40,)), dma((12,)), dma((12,)), dma, dma, dma((6,)), dma((8,)),
+            dma((40,)), dma((40,)), dma((12,)), dma((12,)), dma, dma, dma((8,)),
         ],
         name="gather",
-        compiler_params=params(has_side_effects=True),
-    )(points, charges, projection, skeleton_index, ids)
-    table = pl.pallas_call(
-        functools.partial(table_kernel, leaf_dev, near_dev, far_dev, n_z),
-        out_shape=shape((chips * n_z, 128), jnp.int32),
-        in_specs=[VMEM],
-        out_specs=VMEM,
-        name="table",
-        compiler_params=params(),
-    )(ids_all)
+        compiler_params=params(has_side_effects=True, collective_id=0, vmem_limit_bytes=28 << 20),
+    )(*[pltpu.with_memory_space_constraint(value, pltpu.HBM) for value in (points, charges, projection, skeleton_index, ids)])
+    tables = [table, y_table, x_aug.reshape(targets, 64, cols), w_table]
     partial_sums = pl.pallas_call(
         pair_kernel,
         out_shape=shape((targets, rhs, cols), F32),
-        in_specs=[SMEM] + [ANY] * 5,
+        in_specs=[VMEM] * 4,
         out_specs=ANY,
         scratch_shapes=[
-            pltpu.VMEM((targets, 64, cols), BF16),
-            pltpu.VMEM((3 * sources, skel, 128), BF16),
-            pltpu.VMEM((3 * sources, rhs, skel), BF16),
             pltpu.VMEM((targets + 1, rhs, cols), F32),
             pltpu.VMEM((DUOS, skel, 2 * cols), F32),
             pltpu.VMEM((DUOS, skel, 2 * cols), F32),
+            pltpu.SMEM((chips * n_z, 128), jnp.int32),
             pltpu.SMEM((chips * n_z * (2 * NEAR_SLOTS + FAR_SLOTS) + 8 * DUOS,), jnp.int32),
             pltpu.SMEM((chips,), jnp.int32),
-            dma((8,)),
             dma,
         ],
         name="pairs",
-        compiler_params=params(),
-    )(table, y_table, x_aug.reshape(targets, 64, cols), w_skel, charges, charges_sib)
+        compiler_params=params(vmem_limit_bytes=28 << 20),
+    )(*[pltpu.with_memory_space_constraint(value, pltpu.VMEM) for value in tables])
     half, part = leaf_dev // 2, leaf_dev // 4
     return pl.pallas_call(
         reduce_kernel,
@@ -702,7 +683,7 @@
             dma((32,)), dma((40,)), dma((40,)), dma((40,)), dma((40,)),
         ],
         name="reduce",
-        compiler_params=params(has_side_effects=True),
+        compiler_params=params(has_side_effects=True, collective_id=1, vmem_limit_bytes=LIMIT),
     )(partial_sums.reshape(chips, leaf_dev, rhs, cols))
 
 

time: 165 us -> 138 us (0.84)
  Pallas kernels: 159 us -> 134 us
    pallas_call x2 -> x1, Pallas kernels: 54.4 us -> 44.8 us  [per_device(): pl.pallas_call(functools.partial(gather_kernel, near_dev, far_dev), out_s...]
    pallas_call x1, Pallas kernels: 59.1 us -> 51.1 us  [per_device(): pl.pallas_call(reduce_kernel, out_shape=shape((leaf_dev, rhs, cols), F32)...]
    pallas_call x1, Pallas kernels: 45.8 us -> 37.9 us  [per_device(): pl.pallas_call(pair_kernel, out_shape=shape((targets, rhs, cols), F32), i...]
    unnamed x3 -> x1, local copies, waits for them, and re-layouts: 3.83 us -> 2.31 us
where the time goes in v3:
time: 138 us; the launch traced here: 137 us
  Pallas kernels  134 us (97%)
  local copies, waits for them, and re-layouts  2.91 us (2%)
    pallas_call x1, Pallas kernels, per_device(): pl.pallas_call(reduce_kernel, out_shape=shape((leaf_dev, rhs, cols), F32)...  51.1 us
    pallas_call x1, Pallas kernels, per_device(): pl.pallas_call(functools.partial(gather_kernel, near_dev, far_dev), out_s...  44.8 us
    pallas_call x1, Pallas kernels, per_device(): pl.pallas_call(pair_kernel, out_shape=shape((targets, rhs, cols), F32), i...  37.9 us

profile of v3, /device:TPU:0, one launch (start us, length us, event | category | flops | bytes accessed | tf_op | source)
XLA Modules:
  0.0 137.4 jit_solution(2339454495863214894)
XLA Ops:
  0.0 0.7 pad_add_fusion
  0.7 0.6 pad.4.ids
  1.3 44.8 %gather.1 = (bf16[192,256,128]{2,1,0:T(8,128)(2,1)S(1)}, bf16[16,32,64,128]{3,2,1,0:T(8,128)(2,1)S(1)}, bf16[192,64,256]{2,1,0:T(8,128)(2,1)S(1)}, s32[64,128]{1,0:T(8,128)S(1)}) custom-call(bf16[32,32,512]{2,1,0:T(8,128)(2,1)} %points.1, bf16[32,64,512]{2,1,0:T(8,128)(2,1)} %charges.1, bf16[32,64,512]{2,1,0:T(8,128)(2,1)} %projection.1, s32[32,256]{1,0:T(8,128)} %index.1, ...), custom_call_target="tpu_custom_call" | custom-call | tf_op jit(solution)/shard_map/gather/pallas_call | solution.py:626
  46.1 37.9 %pairs.1 = f32[512,64,128]{2,1,0:T(8,128)} custom-call(s32[64,128]{1,0:T(8,128)S(1)} %get-tuple-element.9.table_in, bf16[192,256,128]{2,1,0:T(8,128)(2,1)S(1)} %get-tuple-element.10.y_table, bf16[512,64,128]{2,1,0:T(8,128)(2,1)S(1)} %bitcast.4, bf16[192,64,256]{2,1,0:T(8,128)(2,1)S(1)} %get-tuple-element.12.w_table), custom_call_target="tpu_custom_call" | custom-call | tf_op jit(solution)/shard_map/pairs/pallas_call | solution.py:650
  84.0 51.1 %reduce.1 = f32[32,64,128]{2,1,0:T(8,128)} custom-call(f32[16,32,64,128]{3,2,1,0:T(8,128)} %bitcast.5), custom_call_target="tpu_custom_call" | custom-call | tf_op jit(solution)/shard_map/reduce/pallas_call | solution.py:668
  135.1 2.3 %copy.8 = f32[32,64,128]{2,1,0:T(8,128)} copy(f32[32,64,128]{2,1,0:T(8,128)} %reduce.1) | data formatting | bytes 2097152

commit v4 on v3

--- a/solution.py
+++ b/solution.py
@@ -9,14 +9,12 @@
 from jax.sharding import PartitionSpec as P
 
 MESH = pl.DeviceIdType.MESH
-ANY = pl.BlockSpec(memory_space=pl.ANY)
 HBM = pl.BlockSpec(memory_space=pltpu.HBM)
 VMEM = pl.BlockSpec(memory_space=pltpu.VMEM)
 RING = 4
 NEAR_SLOTS = 6
 FAR_SLOTS = 10
 DUOS = 6
-LIMIT = 62 * 1024 * 1000
 F32 = jnp.float32
 BF16 = jnp.bfloat16
 
@@ -81,13 +79,14 @@
 
 
 def gather_kernel(
-    near_dev, far_dev, points, charges, projection, index, ids,
+    points, charges, projection, index, near_t, far_t,
     y_table, x_aug, w_table, table,
-    ids_all, p_buf, i_buf, c_buf, j_buf, q_buf, x_raw,
+    ids, ids_all, p_buf, i_buf, c_buf, j_buf, q_buf, x_raw,
     send_x, recv_x, send_s, recv_s, send_i, recv_i, load_sems,
 ):
     x, y, core, z = torus_position()
     n_z = q_buf.shape[1]
+    near_dev, far_dev = near_t.shape[0], far_t.shape[0]
     leaf_dev, dim, leaf = points.shape
     skel = index.shape[1]
     cols = x_raw.shape[3]
@@ -122,7 +121,6 @@
             (points, p_buf.at[0]),
             (index, i_buf.at[0]),
             (points.at[:, :, own_cols], x_raw.at[here]),
-            (ids, ids_all.at[me]),
             (charges.at[:, :, pl.ds(0, skel)], w_table.at[pl.ds(0, leaf_dev)]),
             (charges.at[:, :, pl.ds(skel, skel)], w_table.at[pl.ds(2 * leaf_dev, leaf_dev)]),
         )
@@ -130,8 +128,26 @@
         copy = pltpu.make_async_copy(src, dst, load_sems.at[at])
         copy.start()
         loads.append(copy)
+
+    blank = jnp.full(ids.shape, -1, jnp.int32)
+    ids[...] = blank
+    ids[:near_dev, :leaf_dev] = near_t[...]
+    ids[near_dev : near_dev + far_dev, :leaf_dev] = far_t[...]
+
+    loads[0].wait()
+    loads[1].wait()
+
+    def charge(item, carry):
+        parts = []
+        for at in (item, item + hold):
+            parts.append(
+                lax.dot_general(c_buf[at], j_buf[at], (((1,), (1,)), ((), ())), preferred_element_type=F32)
+            )
+        q_buf[0, z, item] = jnp.concatenate(parts, axis=1).astype(BF16)
+        return carry
+
+    lax.fori_loop(0, hold, charge, 0, unroll=2)
     pl.semaphore_wait(barrier, n_ids)
-
     sends = []
 
     def message(kind, sems, src, dst, target):
@@ -190,19 +206,6 @@
 
     lax.fori_loop(1, n_ids, send_ids, 0)
 
-    loads[0].wait()
-    loads[1].wait()
-
-    def charge(item, carry):
-        parts = []
-        for at in (item, item + hold):
-            parts.append(
-                lax.dot_general(c_buf[at], j_buf[at], (((1,), (1,)), ((), ())), preferred_element_type=F32)
-            )
-        q_buf[0, z, item] = jnp.concatenate(parts, axis=1).astype(BF16)
-        return carry
-
-    lax.fori_loop(0, hold, charge, 0, unroll=2)
     z_copies = []
     own_quarter = q_buf.at[0, z]
     for step in range(1, n_z):
@@ -324,6 +327,7 @@
         copy.wait()
     sib_copies[2].wait_recv()
     sib_copies[3].wait_recv()
+    ids_all[me] = ids[...]
     others = ids_all.at[pl.ds(0, n_ids - 1)]
     every = pltpu.make_async_remote_copy(
         src_ref=others, dst_ref=others, send_sem=send_i, recv_sem=recv_i,
@@ -354,8 +358,8 @@
         copy.wait_send()
 
 
-def pair_kernel(table_in, y_table, x_aug, w_table, out, acc, s_a, s_b, table, items, ends, out_sem):
-    copy = pltpu.make_async_copy(table_in, table, out_sem)
+def pair_kernel(table_in, y_table, x_aug, w_table, acc, s_a, s_b, table, items, load_sem):
+    copy = pltpu.make_async_copy(table_in, table, load_sem)
     copy.start()
     skel = y_table.shape[1]
     targets, _, cols = x_aug.shape
@@ -381,7 +385,6 @@
             for slot in range(FAR_SLOTS):
                 items[count + slot] = table[row, NEAR_SLOTS + slot]
             count = count + table[row, NEAR_SLOTS + FAR_SLOTS + 1]
-        ends[chip] = count
         return count
 
     chips = table.shape[0] // n_z
@@ -423,40 +426,23 @@
     for duo in range(DUOS):
         scores(0, s_a, duo)
 
-    def store(chip):
-        rows = pl.ds(pl.multiple_of(chip * leaf_dev, leaf_dev), leaf_dev)
-        return pltpu.make_async_copy(acc.at[rows], out.at[rows], out_sem)
-
-    def step(at, chip):
+    def step(at, carry):
         for duo in range(DUOS):
             sums(2 * at, s_a, duo)
             scores(2 * at + 1, s_b, duo)
         for duo in range(DUOS):
             sums(2 * at + 1, s_b, duo)
             scores(2 * at + 2, s_a, duo)
-        full = jnp.logical_and(chip < chips, ends[jnp.minimum(chip, chips - 1)] <= (at + 1) * 4 * DUOS)
-
-        @pl.when(full)
-        def _():
-            store(chip).start()
-
-        return jnp.where(full, chip + 1, chip)
-
-    def flush(chip, carry):
-        store(chip).start()
         return carry
 
-    chip = lax.fori_loop(0, lax.div(count + 4 * DUOS - 1, 4 * DUOS), step, 0)
-    lax.fori_loop(chip, chips, flush, 0)
-    pltpu.make_async_copy(acc.at[pl.ds(0, targets)], out, out_sem).wait()
+    lax.fori_loop(0, lax.div(count + 4 * DUOS - 1, 4 * DUOS), step, 0)
 
 
 def reduce_kernel(
-    part_all, out, held, send_8, recv_8, send_16, recv_16, scale_s8, scale_r8, scale_s16, scale_r16,
-    load_sems, sem_s8, sem_r8, sem_s16, sem_r16,
+    leaf_dev, held, out, send_8, recv_8, send_16, recv_16, scale_s8, scale_r8, scale_s16, scale_r16,
+    sem_s8, sem_r8, sem_s16, sem_r16,
 ):
     x, y, core, z = torus_position()
-    leaf_dev = part_all.shape[1]
     half, part = leaf_dev // 2, leaf_dev // 4
     order = ((2, 0), (1, 1), (-1, 2), (0, 3))
 
@@ -470,18 +456,6 @@
         pl.semaphore_signal(
             barrier, inc=1, device_id=(chip_at(0, du, dv) * 2 + core, z), device_id_type=MESH
         )
-
-    loads = {}
-    for du, _ in order:
-        for dv, _ in order:
-            for half_at in range(2):
-                slot = chip_at(half_at, du, dv)
-                ref = pl.ds(half_at * half, half)
-                copy = pltpu.make_async_copy(
-                    part_all.at[slot, ref], held.at[slot, ref], load_sems.at[len(loads)]
-                )
-                copy.start()
-                loads[half_at, du, dv] = copy
 
     pl.semaphore_wait(barrier, 4)
     sends = []
@@ -505,7 +479,7 @@
         data, scale = (recv_16, scale_r16) if size == half else (recv_8, scale_r8)
         return data[kind, row].astype(jnp.int32).astype(F32) * scale[kind, pl.ds(row, 1), :]
 
-    def send(size, kind, chip, value_at):
+    def code(size, kind, first, count, value_at):
         data, scale = (send_16, scale_s16) if size == half else (send_8, scale_s8)
 
         def body(row, carry):
@@ -515,7 +489,9 @@
             data[kind, row] = jnp.round(value * (32767.0 / top)).astype(jnp.int32).astype(jnp.int16)
             return carry
 
-        lax.fori_loop(0, size, body, 0, unroll=2)
+        lax.fori_loop(first, first + count, body, 0, unroll=2)
+
+    def send(size, kind, chip):
         for copy in wires(size, kind, chip):
             copy.start()
             sends.append(copy)
@@ -524,81 +500,67 @@
         for copy in wires(size, kind, chip_at(0, 1, 0)):
             copy.wait_recv()
 
-    def ready(half_at, du, dv):
-        loads.pop((half_at, du, dv)).wait()
+    def local(half_at, du, dv):
+        start = chip_at(half_at, du, dv) * leaf_dev + half_at * half
+        return lambda row: held[start + row]
 
     for dv, at in order:
         for half_at in range(2):
-            base = half_at * half
-            ready(half_at, 2, dv)
-            slot = chip_at(half_at, 2, dv)
             kind = half_at * 10 + 2 * at
-            send(part, kind, chip_at(half_at, 1, 0), lambda row: held[slot, base + row])
-            send(part, kind + 1, chip_at(half_at, -1, 0), lambda row: held[slot, base + part + row])
+            mine = local(half_at, 2, dv)
+            for side, du in ((0, 1), (1, -1)):
+                code(part, kind + side, 0, part, lambda row: mine(side * part + row))
+                send(part, kind + side, chip_at(half_at, du, 0))
+
+    def add_part(kind, side, mine):
+        wait(part, kind)
+        low = side * part
+        code(half, kind, low, part, lambda row: mine(row) + unpack(part, kind, row - low))
+
     def pass_on(dv, at):
         for half_at in range(2):
-            base = half_at * half
             for du, side in ((1, 0), (-1, 1)):
-                ready(half_at, du, dv)
-                slot = chip_at(half_at, du, dv)
                 kind = half_at * 10 + 2 * at + side
-                wait(part, kind)
-
-                def add(row, carry):
-                    spot = base + side * part + row
-                    held[slot, spot] = held[slot, spot] + unpack(part, kind, row)
-                    return carry
-
-                lax.fori_loop(0, part, add, 0, unroll=2)
-                send(half, kind, chip_at(half_at, du, 0), lambda row: held[slot, base + row])
+                mine = local(half_at, du, dv)
+                code(half, kind, part - side * part, part, mine)
+                add_part(kind, side, mine)
+                send(half, kind, chip_at(half_at, du, 0))
+
+    def column(half_at, dv, at):
+        kind = half_at * 10 + 2 * at
+        mine = local(half_at, 0, dv)
+        wait(half, kind)
+        wait(half, kind + 1)
+        return lambda row: mine(row) + unpack(half, kind, row) + unpack(half, kind + 1, row)
 
     def second_axis(dv, at):
         for half_at in range(2):
-            base = half_at * half
-            ready(half_at, 0, dv)
-            slot = chip_at(half_at, 0, dv)
-            kind = half_at * 10 + 2 * at
-            wait(half, kind)
-            wait(half, kind + 1)
-
-            def keep(row, carry):
-                held[slot, base + row] = held[slot, base + row] + unpack(half, kind, row) + unpack(half, kind + 1, row)
-                return carry
-
-            lax.fori_loop(0, half, keep, 0, unroll=2)
+            total = column(half_at, dv, at)
             if dv == 2:
                 for sign, side in ((1, 0), (-1, 1)):
-                    send(
-                        part, half_at * 10 + 8 + side, chip_at(half_at, 0, sign),
-                        lambda row: held[slot, base + side * part + row],
-                    )
-            elif dv != 0:
+                    late = half_at * 10 + 8 + side
+                    code(part, late, 0, part, lambda row: total(side * part + row))
+                    send(part, late, chip_at(half_at, 0, sign))
+            else:
                 side = 0 if dv == 1 else 1
                 late = half_at * 10 + 8 + side
-                wait(part, late)
-
-                def add_late(row, carry):
-                    spot = base + side * part + row
-                    held[slot, spot] = held[slot, spot] + unpack(part, late, row)
-                    return carry
-
-                lax.fori_loop(0, part, add_late, 0, unroll=2)
-                send(half, late, chip_at(half_at, 0, dv), lambda row: held[slot, base + row])
+                code(half, late, part - side * part, part, total)
+                add_part(late, side, total)
+                send(half, late, chip_at(half_at, 0, dv))
 
     for step, (dv, at) in enumerate(order):
         pass_on(dv, at)
         if step > 0:
             second_axis(*order[step - 1])
-    second_axis(*order[-1])
     for half_at in range(2):
         base = half_at * half
-        slot = chip_at(half_at, 0, 0)
+        total = column(half_at, *order[-1])
         kind = half_at * 10 + 8
         wait(half, kind)
         wait(half, kind + 1)
 
         def finish(row, carry):
-            out[base + row] = held[slot, base + row] + unpack(half, kind, row) + unpack(half, kind + 1, row)
+            out[base + row] = total(row) + unpack(half, kind, row) + unpack(half, kind + 1, row)
             return carry
 
         lax.fori_loop(0, half, finish, 0, unroll=2)
@@ -619,21 +581,19 @@
     dma = pltpu.SemaphoreType.DMA
     shape = jax.ShapeDtypeStruct
 
-    ids = jnp.concatenate([near_ids.T, far_ids.T], axis=0)
-    ids = jnp.pad(ids, ((0, 8 - near_dev - far_dev), (0, 128 - leaf_dev)), constant_values=-1)
-
     quarter = (leaf_dev // 2, rhs, 2 * skel // n_z)
     y_table, x_aug, w_table, table = pl.pallas_call(
-        functools.partial(gather_kernel, near_dev, far_dev),
+        gather_kernel,
         out_shape=[
             pltpu.VMEM((3 * sources, skel, 128), BF16),
             pltpu.VMEM((chips, leaf_dev, 64, cols), BF16),
             pltpu.VMEM((3 * sources, rhs, skel), BF16),
             pltpu.VMEM((chips * n_z, 128), jnp.int32),
         ],
-        in_specs=[HBM] * 5,
+        in_specs=[HBM] * 4 + [VMEM] * 2,
         out_specs=[VMEM] * 4,
         scratch_shapes=[
+            pltpu.VMEM((8, 128), jnp.int32),
             pltpu.VMEM((chips * n_z, 8, 128), jnp.int32),
             pltpu.VMEM((2,) + points.shape, BF16),
             pltpu.VMEM((2,) + skeleton_index.shape, jnp.int32),
@@ -644,34 +604,38 @@
             dma((40,)), dma((40,)), dma((12,)), dma((12,)), dma, dma, dma((8,)),
         ],
         name="gather",
-        compiler_params=params(has_side_effects=True, collective_id=0, vmem_limit_bytes=28 << 20),
-    )(*[pltpu.with_memory_space_constraint(value, pltpu.HBM) for value in (points, charges, projection, skeleton_index, ids)])
+        compiler_params=params(has_side_effects=True, collective_id=0, vmem_limit_bytes=17 << 20),
+    )(
+        *[
+            pltpu.with_memory_space_constraint(value, pltpu.HBM)
+            for value in (points, charges, projection, skeleton_index)
+        ],
+        near_ids.T,
+        far_ids.T,
+    )
     tables = [table, y_table, x_aug.reshape(targets, 64, cols), w_table]
     partial_sums = pl.pallas_call(
         pair_kernel,
-        out_shape=shape((targets, rhs, cols), F32),
+        out_shape=pltpu.VMEM((targets + 1, rhs, cols), F32),
         in_specs=[VMEM] * 4,
-        out_specs=ANY,
+        out_specs=VMEM,
         scratch_shapes=[
-            pltpu.VMEM((targets + 1, rhs, cols), F32),
             pltpu.VMEM((DUOS, skel, 2 * cols), F32),
             pltpu.VMEM((DUOS, skel, 2 * cols), F32),
             pltpu.SMEM((chips * n_z, 128), jnp.int32),
             pltpu.SMEM((chips * n_z * (2 * NEAR_SLOTS + FAR_SLOTS) + 8 * DUOS,), jnp.int32),
-            pltpu.SMEM((chips,), jnp.int32),
             dma,
         ],
         name="pairs",
-        compiler_params=params(vmem_limit_bytes=28 << 20),
+        compiler_params=params(vmem_limit_bytes=6 << 20),
     )(*[pltpu.with_memory_space_constraint(value, pltpu.VMEM) for value in tables])
     half, part = leaf_dev // 2, leaf_dev // 4
     return pl.pallas_call(
-        reduce_kernel,
-        out_shape=shape((leaf_dev, rhs, cols), F32),
-        in_specs=[ANY],
+        functools.partial(reduce_kernel, leaf_dev),
+        out_shape=pltpu.VMEM((leaf_dev, rhs, cols), F32),
+        in_specs=[VMEM],
         out_specs=VMEM,
         scratch_shapes=[
-            pltpu.VMEM((chips, leaf_dev, rhs, cols), F32),
             pltpu.VMEM((20, part, rhs, cols), jnp.int16),
             pltpu.VMEM((20, part, rhs, cols), jnp.int16),
             pltpu.VMEM((20, half, rhs, cols), jnp.int16),
@@ -680,11 +644,11 @@
             pltpu.VMEM((20, part, cols), F32),
             pltpu.VMEM((20, half, cols), F32),
             pltpu.VMEM((20, half, cols), F32),
-            dma((32,)), dma((40,)), dma((40,)), dma((40,)), dma((40,)),
+            dma((40,)), dma((40,)), dma((40,)), dma((40,)),
         ],
         name="reduce",
-        compiler_params=params(has_side_effects=True, collective_id=1, vmem_limit_bytes=LIMIT),
-    )(partial_sums.reshape(chips, leaf_dev, rhs, cols))
+        compiler_params=params(has_side_effects=True, collective_id=1, vmem_limit_bytes=17 << 20),
+    )(pltpu.with_memory_space_constraint(partial_sums, pltpu.VMEM))
 
 
 def solution(mesh):

time: 138 us -> 135 us (0.978)
  Pallas kernels: 134 us -> 132 us
    pallas_call x3, Pallas kernels: 134 us -> 132 us  [the longest x1 49.8 us: per_device(): pl.pallas_call(functools.partial(reduce_kernel, leaf_dev), out_shape=pltp...]
where the time goes in v4:
time: 135 us
  Pallas kernels  132 us (98%)
  local copies, waits for them, and re-layouts  2.33 us (2%)
    pallas_call x1, Pallas kernels, per_device(): pl.pallas_call(functools.partial(reduce_kernel, leaf_dev), out_shape=pltp...  49.8 us
    pallas_call x1, Pallas kernels, per_device(): pl.pallas_call(gather_kernel, out_shape=[pltpu.VMEM((3 * sources, skel, 1...  43.7 us
    pallas_call x1, Pallas kernels, per_device(): pl.pallas_call(pair_kernel, out_shape=pltpu.VMEM((targets + 1, rhs, cols)...  38.7 us

profile of v4, /device:TPU:0, one launch (start us, length us, event | category | flops | bytes accessed | tf_op | source)
XLA Modules:
  0.0 134.6 jit_solution(1774576667827835480)
XLA Ops:
  0.0 0.0 copy-start
  0.0 0.7 copy-done
  0.7 0.0 copy-start.1
  0.7 0.7 copy-done.1
  1.4 43.7 %gather.1 = (bf16[192,256,128]{2,1,0:T(8,128)(2,1)S(1)}, bf16[16,32,64,128]{3,2,1,0:T(8,128)(2,1)S(1)}, bf16[192,64,256]{2,1,0:T(8,128)(2,1)S(1)}, s32[64,128]{1,0:T(8,128)S(1)}) custom-call(bf16[32,32,512]{2,1,0:T(8,128)(2,1)} %points.1, bf16[32,64,512]{2,1,0:T(8,128)(2,1)} %charges.1, bf16[32,64,512]{2,1,0:T(8,128)(2,1)} %projection.1, s32[32,256]{1,0:T(8,128)} %index.1, ...), custom_call_target="tpu_custom_call" | custom-call | tf_op jit(solution)/shard_map/gather/pallas_call | solution.py:585
  45.1 38.7 %pairs.1.held = f32[513,64,128]{2,1,0:T(8,128)S(1)} custom-call(s32[64,128]{1,0:T(8,128)S(1)} %get-tuple-element.9.table_in, bf16[192,256,128]{2,1,0:T(8,128)(2,1)S(1)} %get-tuple-element.10.y_table, bf16[512,64,128]{2,1,0:T(8,128)(2,1)S(1)} %bitcast.3, bf16[192,64,256]{2,1,0:T(8,128)(2,1)S(1)} %get-tuple-element.12.w_table), custom_call_target="tpu_custom_call" | custom-call | tf_op jit(solution)/shard_map/pairs/pallas_call | solution.py:617
  83.8 49.8 %reduce.1 = f32[32,64,128]{2,1,0:T(8,128)S(1)} custom-call(f32[513,64,128]{2,1,0:T(8,128)S(1)} %pairs.1.held), custom_call_target="tpu_custom_call" | custom-call | tf_op jit(solution)/shard_map/reduce/pallas_call | solution.py:633
  133.6 1.0 copy.8
Async XLA Ops:
  0.0 0.7 copy-start
  0.7 0.7 copy-start.1

commit v5 on v4

--- a/solution.py
+++ b/solution.py
@@ -79,9 +79,9 @@
 
 
 def gather_kernel(
-    points, charges, projection, index, near_t, far_t,
+    points, charges, projection, index, near_in, far_in,
     y_table, x_aug, w_table, table,
-    ids, ids_all, p_buf, i_buf, c_buf, j_buf, q_buf, x_raw,
+    near_t, far_t, ids, ids_all, p_buf, i_buf, c_buf, j_buf, q_buf, x_raw,
     send_x, recv_x, send_s, recv_s, send_i, recv_i, load_sems,
 ):
     x, y, core, z = torus_position()
@@ -103,14 +103,15 @@
 
     barrier = pltpu.get_barrier_semaphore()
 
-    def greet(step, carry):
-        peer = lax.rem(me + step, n_ids)
-        pl.semaphore_signal(
-            barrier, inc=1, device_id=device(peer // n_z, core, lax.rem(peer, n_z)), device_id_type=MESH
-        )
-        return carry
-
-    lax.fori_loop(1, n_ids, greet, 0)
+    peers = []
+    for dx in range(RING):
+        for dy in range(RING):
+            chip = wrap(x + dx) * RING + wrap(y + dy)
+            for dz in range(n_z):
+                if dx or dy or dz:
+                    peers.append(device(chip, core, lax.rem(z + dz, n_z)))
+    for peer in peers:
+        pl.semaphore_signal(barrier, inc=1, device_id=peer, device_id_type=MESH)
     pl.semaphore_signal(barrier, inc=1, device_id=device(here, 1 - core, z), device_id_type=MESH)
 
     loads = []
@@ -123,6 +124,8 @@
             (points.at[:, :, own_cols], x_raw.at[here]),
             (charges.at[:, :, pl.ds(0, skel)], w_table.at[pl.ds(0, leaf_dev)]),
             (charges.at[:, :, pl.ds(skel, skel)], w_table.at[pl.ds(2 * leaf_dev, leaf_dev)]),
+            (near_in, near_t),
+            (far_in, far_t),
         )
     ):
         copy = pltpu.make_async_copy(src, dst, load_sems.at[at])
@@ -131,6 +134,8 @@
 
     blank = jnp.full(ids.shape, -1, jnp.int32)
     ids[...] = blank
+    loads[7].wait()
+    loads[8].wait()
     ids[:near_dev, :leaf_dev] = near_t[...]
     ids[near_dev : near_dev + far_dev, :leaf_dev] = far_t[...]
 
@@ -196,16 +201,6 @@
         start(copy)
         sib_copies.append(copy)
 
-    def send_ids(step, carry):
-        peer = lax.rem(me + step, n_ids)
-        pltpu.make_async_remote_copy(
-            src_ref=ids, dst_ref=ids_all.at[me], send_sem=send_i, recv_sem=recv_i,
-            device_id=device(peer // n_z, core, lax.rem(peer, n_z)), device_id_type=MESH,
-        ).start()
-        return carry
-
-    lax.fori_loop(1, n_ids, send_ids, 0)
-
     z_copies = []
     own_quarter = q_buf.at[0, z]
     for step in range(1, n_z):
@@ -215,6 +210,12 @@
     copy = message(0, side, own_quarter, q_buf.at[1, z], device(here, 1 - core, z))
     start(copy)
     sib_quarters = [copy]
+
+    for peer in peers:
+        pltpu.make_async_remote_copy(
+            src_ref=ids, dst_ref=ids_all.at[me], send_sem=send_i, recv_sem=recv_i,
+            device_id=peer, device_id_type=MESH,
+        ).start()
 
     def item(half_at, du, dv, quarter_at=None):
         first_x = half_at == 0
@@ -278,7 +279,7 @@
             y_table[2 * sources + row] = picked.T
             return carry
 
-        lax.fori_loop(first, first + count, body, 0, unroll=2)
+        lax.fori_loop(first, first + count, body, 0, unroll=4)
 
     def assemble(at_side):
         def body(at, carry):
@@ -290,6 +291,9 @@
 
         lax.fori_loop(0, hold, body, 0, unroll=2)
 
+    for copy in loads[2:5]:
+        copy.wait()
+    source(0, 0, leaf_dev // 2)
     for half_at in range(2):
         arrived(half_at, 0, item(half_at, -1, 0))
         forward(half_at, 2, item(half_at, -1, 0, 0), 1, 0)
@@ -298,35 +302,40 @@
         arrived(half_at, 1, item(half_at, 1, 0))
         forward(half_at, 3, item(half_at, 1, 0, 1), -1, 0)
         across(half_at, 2, 1)
+    source(0, leaf_dev // 2, leaf_dev // 2)
     for half_at in range(2):
         relay(half_at, 0, 0)
-    loads[2].wait()
-    loads[3].wait()
-    loads[4].wait()
-    source(0, 0, leaf_dev // 2)
-    for half_at in range(2):
-        arrived(half_at, 2, item(half_at, 2, 0, 0))
-        arrived(half_at, 3, item(half_at, 2, 0, 1))
-        across(half_at, 3, 2)
     for step in range(1, n_z):
         z_copies[step - 1].wait_recv()
         slot = lax.rem(z - step + n_z, n_z)
         copy = message(4 + step, side, q_buf.at[0, slot], q_buf.at[1, slot], device(here, 1 - core, z))
         start(copy)
         sib_quarters.append(copy)
-    source(0, leaf_dev // 2, leaf_dev // 2)
-    for half_at in range(2):
-        relay(half_at, 1, -1)
     sib_copies[0].wait_recv()
     sib_copies[1].wait_recv()
     source(1, 0, leaf_dev // 2)
     for half_at in range(2):
+        arrived(half_at, 2, item(half_at, 2, 0, 0))
+        arrived(half_at, 3, item(half_at, 2, 0, 1))
+        across(half_at, 3, 2)
+    source(1, leaf_dev // 2, leaf_dev // 2)
+    for half_at in range(2):
+        relay(half_at, 1, -1)
+    for half_at in range(2):
+        for du in (0, -1, 1, 2):
+            widen(half_at, du, 0)
+    for half_at in range(2):
         relay(half_at, 2, 1)
-    source(1, leaf_dev // 2, leaf_dev // 2)
-    for copy in loads[5:]:
+    for copy in loads[5:7]:
         copy.wait()
     sib_copies[2].wait_recv()
     sib_copies[3].wait_recv()
+    assemble(0)
+    for copy in sib_quarters:
+        copy.wait_recv()
+    assemble(1)
+    for half_at in range(2):
+        relay(half_at, 3, 2)
     ids_all[me] = ids[...]
     others = ids_all.at[pl.ds(0, n_ids - 1)]
     every = pltpu.make_async_remote_copy(
@@ -336,15 +345,6 @@
     every.wait_send()
     every.wait_recv()
     table[...] = chip_table(leaf_dev, near_dev, far_dev, n_z, here, core, ids_all)
-    for half_at in range(2):
-        for du in (0, -1, 1, 2):
-            widen(half_at, du, 0)
-    for half_at in range(2):
-        relay(half_at, 3, 2)
-    assemble(0)
-    for copy in sib_quarters:
-        copy.wait_recv()
-    assemble(1)
     for half_at in range(2):
         for dv in (-1, 1):
             for du in (0, -1, 1, 2):
@@ -590,9 +590,11 @@
             pltpu.VMEM((3 * sources, rhs, skel), BF16),
             pltpu.VMEM((chips * n_z, 128), jnp.int32),
         ],
-        in_specs=[HBM] * 4 + [VMEM] * 2,
+        in_specs=[HBM] * 6,
         out_specs=[VMEM] * 4,
         scratch_shapes=[
+            pltpu.VMEM((near_dev, leaf_dev), jnp.int32),
+            pltpu.VMEM((far_dev, leaf_dev), jnp.int32),
             pltpu.VMEM((8, 128), jnp.int32),
             pltpu.VMEM((chips * n_z, 8, 128), jnp.int32),
             pltpu.VMEM((2,) + points.shape, BF16),
@@ -601,17 +603,15 @@
             pltpu.VMEM(projection.shape, BF16),
             pltpu.VMEM((2, n_z) + quarter, BF16),
             pltpu.VMEM((chips, leaf_dev, dim, cols), BF16),
-            dma((40,)), dma((40,)), dma((12,)), dma((12,)), dma, dma, dma((8,)),
+            dma((40,)), dma((40,)), dma((12,)), dma((12,)), dma, dma, dma((9,)),
         ],
         name="gather",
         compiler_params=params(has_side_effects=True, collective_id=0, vmem_limit_bytes=17 << 20),
     )(
         *[
             pltpu.with_memory_space_constraint(value, pltpu.HBM)
-            for value in (points, charges, projection, skeleton_index)
-        ],
-        near_ids.T,
-        far_ids.T,
+            for value in (points, charges, projection, skeleton_index, near_ids.T, far_ids.T)
+        ]
     )
     tables = [table, y_table, x_aug.reshape(targets, 64, cols), w_table]
     partial_sums = pl.pallas_call(

time: 135 us -> 127 us (0.941)
  Pallas kernels: 132 us -> 126 us
  local copies, waits for them, and re-layouts: 2.33 us -> 0.97 us
    pallas_call x1, Pallas kernels: 43.7 us -> 39.9 us  [per_device(): pl.pallas_call(gather_kernel, out_shape=[pltpu.VMEM((3 * sources, skel, 1...]
    pallas_call x1, Pallas kernels: 49.8 us -> 48.2 us  [per_device(): pl.pallas_call(functools.partial(reduce_kernel, leaf_dev), out_shape=pltp...]
    unnamed x5 -> x1, local copies, waits for them, and re-layouts: 2.33 us -> 0.97 us
where the time goes in v5:
time: 127 us
  Pallas kernels  126 us (99%)
    pallas_call x1, Pallas kernels, per_device(): pl.pallas_call(functools.partial(reduce_kernel, leaf_dev), out_shape=pltp...  48.2 us
    pallas_call x1, Pallas kernels, per_device(): pl.pallas_call(gather_kernel, out_shape=[pltpu.VMEM((3 * sources, skel, 1...  39.9 us
    pallas_call x1, Pallas kernels, per_device(): pl.pallas_call(pair_kernel, out_shape=pltpu.VMEM((targets + 1, rhs, cols)...  37.8 us

profile of v5, /device:TPU:0, one launch (start us, length us, event | category | flops | bytes accessed | tf_op | source)
XLA Modules:
  0.0 126.9 jit_solution(9862993775935209490)
XLA Ops:
  0.0 39.9 %gather.1 = (bf16[192,256,128]{2,1,0:T(8,128)(2,1)S(1)}, bf16[16,32,64,128]{3,2,1,0:T(8,128)(2,1)S(1)}, bf16[192,64,256]{2,1,0:T(8,128)(2,1)S(1)}, s32[64,128]{1,0:T(8,128)S(1)}) custom-call(bf16[32,32,512]{2,1,0:T(8,128)(2,1)} %points.1, bf16[32,64,512]{2,1,0:T(8,128)(2,1)} %charges.1, bf16[32,64,512]{2,1,0:T(8,128)(2,1)} %projection.1, s32[32,256]{1,0:T(8,128)} %index.1, ...), custom_call_target="tpu_custom_call" | custom-call | tf_op jit(solution)/shard_map/gather/pallas_call | solution.py:585
  39.9 37.8 %pairs.1.held = f32[513,64,128]{2,1,0:T(8,128)S(1)} custom-call(s32[64,128]{1,0:T(8,128)S(1)} %get-tuple-element.9.table_in, bf16[192,256,128]{2,1,0:T(8,128)(2,1)S(1)} %get-tuple-element.10.y_table, bf16[512,64,128]{2,1,0:T(8,128)(2,1)S(1)} %bitcast.3, bf16[192,64,256]{2,1,0:T(8,128)(2,1)S(1)} %get-tuple-element.12.w_table), custom_call_target="tpu_custom_call" | custom-call | tf_op jit(solution)/shard_map/pairs/pallas_call | solution.py:617
  77.7 48.2 %reduce.1 = f32[32,64,128]{2,1,0:T(8,128)S(1)} custom-call(f32[513,64,128]{2,1,0:T(8,128)S(1)} %pairs.1.held), custom_call_target="tpu_custom_call" | custom-call | tf_op jit(solution)/shard_map/reduce/pallas_call | solution.py:633
  125.9 1.0 copy.8

commit v6 on v5

--- a/solution.py
+++ b/solution.py
@@ -14,7 +14,7 @@
 RING = 4
 NEAR_SLOTS = 6
 FAR_SLOTS = 10
-DUOS = 6
+DUOS = 8
 F32 = jnp.float32
 BF16 = jnp.bfloat16
 
@@ -367,14 +367,12 @@
     n_z = table.shape[0] // (targets // leaf_dev)
     sources = 2 * leaf_dev
 
-    def zero(at, carry):
-        acc[at] = jnp.zeros(acc.shape[1:], F32)
-        return carry
-
-    lax.fori_loop(0, targets + 1, zero, 0, unroll=4)
+    blank = jnp.zeros((leaf_dev,) + acc.shape[1:], F32)
+    acc[targets] = blank[0]
     copy.wait()
 
     def fill(chip, count):
+        acc[pl.ds(pl.multiple_of(chip * leaf_dev, leaf_dev), leaf_dev)] = blank
         for step in range(n_z):
             row = chip * n_z + step
             for slot in range(NEAR_SLOTS):

time: 127 us -> 128 us (level)
    pallas_call x1, Pallas kernels: 48.2 us -> 49.5 us  [per_device(): pl.pallas_call(functools.partial(reduce_kernel, leaf_dev), out_shape=pltp...]
where the time goes in v6:
time: 128 us
  Pallas kernels  127 us (99%)
    pallas_call x1, Pallas kernels, per_device(): pl.pallas_call(functools.partial(reduce_kernel, leaf_dev), out_shape=pltp...  49.5 us
    pallas_call x1, Pallas kernels, per_device(): pl.pallas_call(gather_kernel, out_shape=[pltpu.VMEM((3 * sources, skel, 1...  39.9 us
    pallas_call x1, Pallas kernels, per_device(): pl.pallas_call(pair_kernel, out_shape=pltpu.VMEM((targets + 1, rhs, cols)...  37.4 us

profile of v6, /device:TPU:0, one launch (start us, length us, event | category | flops | bytes accessed | tf_op | source)
XLA Modules:
  0.0 127.8 jit_solution(4273177955526610891)
XLA Ops:
  0.0 39.9 %gather.1 = (bf16[192,256,128]{2,1,0:T(8,128)(2,1)S(1)}, bf16[16,32,64,128]{3,2,1,0:T(8,128)(2,1)S(1)}, bf16[192,64,256]{2,1,0:T(8,128)(2,1)S(1)}, s32[64,128]{1,0:T(8,128)S(1)}) custom-call(bf16[32,32,512]{2,1,0:T(8,128)(2,1)} %points.1, bf16[32,64,512]{2,1,0:T(8,128)(2,1)} %charges.1, bf16[32,64,512]{2,1,0:T(8,128)(2,1)} %projection.1, s32[32,256]{1,0:T(8,128)} %index.1, ...), custom_call_target="tpu_custom_call" | custom-call | tf_op jit(solution)/shard_map/gather/pallas_call | solution.py:583
  39.9 37.4 %pairs.1.held = f32[513,64,128]{2,1,0:T(8,128)S(1)} custom-call(s32[64,128]{1,0:T(8,128)S(1)} %get-tuple-element.9.table_in, bf16[192,256,128]{2,1,0:T(8,128)(2,1)S(1)} %get-tuple-element.10.y_table, bf16[512,64,128]{2,1,0:T(8,128)(2,1)S(1)} %bitcast.3, bf16[192,64,256]{2,1,0:T(8,128)(2,1)S(1)} %get-tuple-element.12.w_table), custom_call_target="tpu_custom_call" | custom-call | tf_op jit(solution)/shard_map/pairs/pallas_call | solution.py:615
  77.3 49.5 %reduce.1 = f32[32,64,128]{2,1,0:T(8,128)S(1)} custom-call(f32[513,64,128]{2,1,0:T(8,128)S(1)} %pairs.1.held), custom_call_target="tpu_custom_call" | custom-call | tf_op jit(solution)/shard_map/reduce/pallas_call | solution.py:631
  126.8 1.0 copy.8
